TPU v7x, 32 devices: a whole 2x2x4 slice. The times are simulated.
32 devices in a mesh: grp: 4 (over y, x), row: 8 (over z, core).
Axes of the slice: x: 2, y: 2, z: 4, core: 2. Of those that a mesh axis runs over, the one named last changes fastest.
Arguments:
- a_tiles: bfloat16 [64, 4, 7, 128, 128], P('row', 'grp'), may hold values from -0.5 to 0.5
- a_cols: int32 [64, 4, 7], P('row', 'grp'), may hold values from 0 to 63, as said below
- p_tiles: bfloat16 [64, 4, 128, 128], P('row'), may hold values from -0.5 to 0.5
- p_cols: int32 [64, 4], replicated, may hold values from 0 to 31, as said below
- c_cols: int32 [32, 16], replicated, may hold values from 0 to 31, as said below
Outputs:
- coarse: float32 [32, 16, 128, 128], P('row', 'grp')
Inputs may be any that keep to these rules, and one draw needn't show every extreme that they name: For fine tile row i in block b = i // 8, every entry of a_cols[i] lies in [max(b - 2, 0) * 8, min(b + 3, 8) * 8). For fine tile row i in block b = i // 8, the entries of p_cols[i] are distinct and lie in [(b - 1) * 4, (b + 2) * 4). For coarse tile row c in block t = c // 4, the entries of c_cols[c] are distinct and lie among the 20 coarse tile rows that start at min(max(t - 2, 0), 3) * 4.
All inputs are finite; a program needn't handle non-finite values.
Results may differ from a plain program's by a relative error of at most 0.0003.
Values may be sent and summed in bfloat16 or wider, within the bound.
A program may use at most 128 MiB of HBM per device.

v0:
```python
import functools

import jax
import jax.numpy as jnp
from jax import lax
from jax.experimental import pallas as pl
from jax.experimental.pallas import tpu as pltpu
from jax.sharding import PartitionSpec as P

RATIO = 2
REACH = 2


LEVELS = 32767.0


def encoded(value):
    most = jnp.maximum(jnp.max(jnp.abs(value), axis=0, keepdims=True), 2e-34)
    code = jnp.round(value * (LEVELS / most)).astype(jnp.int32).astype(jnp.int16)
    return code, most * (1.0 / LEVELS)


def decoded(code, scale):
    return code.astype(jnp.int32).astype(jnp.float32) * scale


def product_kernel(
    sizes,
    where,
    a_cols,
    p_cols,
    c_cols,
    a_ref,
    band_ref,
    center_ref,
    codes_ref,
    scales_ref,
    total_ref,
    spread,
    halves,
):
    fine_rows, slots, kp, kc, tile, chunks = sizes
    coarse_rows = fine_rows // RATIO
    window = (2 * (REACH + 1) + 1) * coarse_rows
    position = where[0]
    first_row = position * fine_rows
    band_start = first_row - REACH * fine_rows
    window_start = (position - REACH - 1) * coarse_rows
    base_coarse = (position - 1) * coarse_rows
    total_ref[...] = jnp.zeros_like(total_ref)
    halves[window] = jnp.zeros((2 * tile, tile), jnp.bfloat16)
    group = min(4, kc)

    @pl.loop(0, fine_rows)
    def _(i):
        spread[...] = jnp.zeros_like(spread)
        for s in range(slots):
            j = a_cols[i * slots + s]
            local = (j - band_start) * kp
            right = jnp.concatenate([band_ref[local + p] for p in range(kp)], axis=1)
            prod = jnp.dot(a_ref[i * slots + s], right, preferred_element_type=jnp.float32)
            for p in range(kp):
                w = p_cols[j * kp + p] - window_start
                spread[w] = spread[w] + prod[:, p * tile : (p + 1) * tile]

        @pl.loop(0, window, unroll=4)
        def _(w):
            value = spread[w]
            high = value.astype(jnp.bfloat16)
            halves[w, :tile] = high
            halves[w, tile:] = (value - high.astype(jnp.float32)).astype(jnp.bfloat16)

        for q in range(kp):
            c = p_cols[(first_row + i) * kp + q]
            own = band_ref[(REACH * fine_rows + i) * kp + q].T
            left = jnp.concatenate([own, own], axis=1)
            out = (c - base_coarse) * kc
            for k in range(0, kc, group):
                parts = []
                for n in range(group):
                    w = c_cols[c * kc + k + n] - window_start
                    w = jnp.where((w < 0) | (w >= window), window, w)
                    parts.append(halves[w])
                prod = jnp.dot(
                    left, jnp.concatenate(parts, axis=1), preferred_element_type=jnp.float32
                )
                for n in range(group):
                    at = out + k + n
                    total_ref[at] = total_ref[at] + prod[:, n * tile : (n + 1) * tile]

    share = kc // chunks
    for chunk in range(chunks):

        @pl.loop(0, coarse_rows)
        def _(c):
            for n in range(share):
                e = c * share + n
                k = chunk * share + n
                center_ref[chunk, e] = total_ref[(coarse_rows + c) * kc + k]
                for side in range(2):
                    value = total_ref[(2 * side * coarse_rows + c) * kc + k]
                    code, scale = encoded(value)
                    codes_ref[side, chunk, e] = code
                    scales_ref[side, chunk, pl.ds(e, 1)] = scale


def local_products(a_tiles, a_cols, band, p_cols, c_cols, position, chunks):
    fine_rows, _, slots, tile, _ = a_tiles.shape
    kp = band.shape[1]
    kc = c_cols.shape[1]
    coarse_rows = fine_rows // RATIO
    window = (2 * (REACH + 1) + 1) * coarse_rows
    members = coarse_rows * kc // chunks
    smem = pl.BlockSpec(memory_space=pltpu.SMEM)
    vmem = pl.BlockSpec(memory_space=pltpu.VMEM)
    return pl.pallas_call(
        functools.partial(product_kernel, (fine_rows, slots, kp, kc, tile, chunks)),
        out_shape=[
            jax.ShapeDtypeStruct((chunks, members, tile, tile), jnp.float32),
            jax.ShapeDtypeStruct((2, chunks, members, tile, tile), jnp.int16),
            jax.ShapeDtypeStruct((2, chunks, members, tile), jnp.float32),
        ],
        in_specs=[smem] * 4 + [vmem] * 2,
        out_specs=[vmem] * 3,
        scratch_shapes=[
            pltpu.VMEM((3 * coarse_rows * kc, tile, tile), jnp.float32),
            pltpu.VMEM((window, tile, tile), jnp.float32),
            pltpu.VMEM((window + 1, 2 * tile, tile), jnp.bfloat16),
        ],
        compiler_params=pltpu.CompilerParams(vmem_limit_bytes=56 * 1024 * 1024),
    )(
        position.reshape(1),
        a_cols.reshape(-1),
        p_cols.reshape(-1),
        c_cols.reshape(-1),
        a_tiles.reshape(-1, tile, tile),
        band.reshape(-1, tile, tile),
    )


def exchange_kernel(
    rows,
    chunks,
    center,
    codes,
    scales,
    out,
    side_codes,
    side_scales,
    sent_codes,
    sent_scales,
    peer_codes,
    peer_scales,
    side_sems,
    side_scale_sems,
    peer_sems,
    peer_scale_sems,
):
    r = lax.axis_index("row")
    g = lax.axis_index("grp")
    members = out.shape[0]
    barrier = pltpu.get_barrier_semaphore()
    mesh_type = pl.DeviceIdType.MESH

    def signal(where):
        pl.semaphore_signal(barrier, inc=1, device_id=where, device_id_type=mesh_type)

    for t in range(chunks - 1):
        signal({"grp": lax.rem(g + 1 + t, chunks)})

    @pl.when(r > 0)
    def _():
        signal({"row": r - 1})

    @pl.when(r < rows - 1)
    def _():
        signal({"row": r + 1})

    inside = (r > 0) & (r < rows - 1)

    @pl.when(inside)
    def _():
        pl.semaphore_wait(barrier, chunks + 1)

    @pl.when(jnp.logical_not(inside))
    def _():
        pl.semaphore_wait(barrier, chunks)

    sends = ((r > 0, r - 1), (r < rows - 1, r + 1))
    comes = (r < rows - 1, r > 0)

    def scale_copy(side):
        return pltpu.make_async_remote_copy(
            src_ref=scales.at[side],
            dst_ref=side_scales.at[side],
            send_sem=side_scale_sems.at[0, side],
            recv_sem=side_scale_sems.at[1, side],
            device_id={"row": sends[side][1]},
            device_id_type=mesh_type,
        )

    def side_copy(side, t):
        return pltpu.make_async_remote_copy(
            src_ref=codes.at[side, lax.rem(g + 1 + t, chunks)],
            dst_ref=side_codes.at[side, t],
            send_sem=side_sems.at[0, side, t],
            recv_sem=side_sems.at[1, side, t],
            device_id={"row": sends[side][1]},
            device_id_type=mesh_type,
        )

    def peer_copy(t):
        return pltpu.make_async_remote_copy(
            src_ref=sent_codes.at[t],
            dst_ref=peer_codes.at[t],
            send_sem=peer_sems.at[0, t],
            recv_sem=peer_sems.at[1, t],
            device_id={"grp": lax.rem(g + 1 + t, chunks)},
            device_id_type=mesh_type,
        )

    def peer_scale_copy(t):
        return pltpu.make_async_remote_copy(
            src_ref=sent_scales.at[t],
            dst_ref=peer_scales.at[t],
            send_sem=peer_scale_sems.at[0, t],
            recv_sem=peer_scale_sems.at[1, t],
            device_id={"grp": lax.rem(g + 1 + t, chunks)},
            device_id_type=mesh_type,
        )

    for side in range(2):

        @pl.when(sends[side][0])
        def _():
            scale_copy(side).start()
            for t in range(chunks):
                side_copy(side, t).start()

        @pl.when(jnp.logical_not(comes[side]))
        def _():
            side_scales[side] = jnp.zeros_like(side_scales[side])

            @pl.loop(0, chunks)
            def _(t):
                @pl.loop(0, members)
                def _(e):
                    side_codes[side, t, e] = jnp.zeros(side_codes.shape[3:], jnp.int16)

    for side in range(2):

        @pl.when(comes[side])
        def _():
            scale_copy(side).wait_recv()

    for t in range(chunks):
        d = lax.rem(g + 1 + t, chunks)
        for side in range(2):

            @pl.when(comes[side])
            def _():
                side_copy(side, t).wait_recv()

        @pl.loop(0, members)
        def _(e):
            value = center[d, e]
            for side in range(2):
                value += decoded(side_codes[side, t, e], side_scales[side, d, pl.ds(e, 1)])
            if t < chunks - 1:
                code, scale = encoded(value)
                sent_codes[t, e] = code
                sent_scales[t, pl.ds(e, 1)] = scale
            else:
                out[e] = value

        if t < chunks - 1:
            peer_scale_copy(t).start()
            peer_copy(t).start()

    for t in range(chunks - 1):
        peer_scale_copy(t).wait_recv()
        peer_copy(t).wait_recv()

        @pl.loop(0, members)
        def _(e):
            out[e] = out[e] + decoded(peer_codes[t, e], peer_scales[t, pl.ds(e, 1)])

    for t in range(chunks - 1):
        peer_scale_copy(t).wait_send()
        peer_copy(t).wait_send()
    for side in range(2):

        @pl.when(sends[side][0])
        def _():
            scale_copy(side).wait_send()
            for t in range(chunks):
                side_copy(side, t).wait_send()


def exchange(center, codes, scales, rows):
    chunks, members, tile, _ = center.shape
    vmem = pl.BlockSpec(memory_space=pltpu.VMEM)
    anywhere = pl.BlockSpec(memory_space=pl.ANY)
    dma = pltpu.SemaphoreType.DMA
    return pl.pallas_call(
        functools.partial(exchange_kernel, rows, chunks),
        out_shape=jax.ShapeDtypeStruct((members, tile, tile), jnp.float32),
        in_specs=[vmem, anywhere, vmem],
        out_specs=vmem,
        scratch_shapes=[
            pltpu.VMEM((2, chunks, members, tile, tile), jnp.int16),
            pltpu.VMEM((2, chunks, members, tile), jnp.float32),
            pltpu.VMEM((chunks - 1, members, tile, tile), jnp.int16),
            pltpu.VMEM((chunks - 1, members, tile), jnp.float32),
            pltpu.VMEM((chunks - 1, members, tile, tile), jnp.int16),
            pltpu.VMEM((chunks - 1, members, tile), jnp.float32),
            dma((2, 2, chunks)),
            dma((2, 2)),
            dma((2, chunks - 1)),
            dma((2, chunks - 1)),
        ],
        compiler_params=pltpu.CompilerParams(
            collective_id=0, has_side_effects=True, vmem_limit_bytes=40 * 1024 * 1024
        ),
    )(center, codes, scales)


def gather_kernel(rows, pieces, own, band, up_sems, down_sems, pair_sems, pass_sems, own_sem):
    r = lax.axis_index("row")
    odd = lax.rem(r, 2)
    partner = r + 1 - 2 * odd
    has_down = r >= 2
    has_up = r < rows - 2
    step = own.shape[0] // pieces
    barrier = pltpu.get_barrier_semaphore()
    mesh_type = pl.DeviceIdType.MESH

    def copy(src, dst, sems, c, to):
        return pltpu.make_async_remote_copy(
            src_ref=src,
            dst_ref=dst,
            send_sem=sems.at[0, c],
            recv_sem=sems.at[1, c],
            device_id={"row": to},
            device_id_type=mesh_type,
        )

    def part(c):
        return pl.ds(c * step, step)

    def up(c):
        return copy(own.at[part(c)], band.at[0, part(c)], up_sems, c, r + 2)

    def down(c):
        return copy(own.at[part(c)], band.at[4, part(c)], down_sems, c, r - 2)

    def pair():
        return copy(own, band.at[1 + 2 * odd], pair_sems, 0, partner)

    def passed(c):
        return copy(
            band.at[4 - 4 * odd, part(c)], band.at[3 - 2 * odd, part(c)], pass_sems, c, partner
        )

    def signal(to):
        pl.semaphore_signal(barrier, inc=1, device_id={"row": to}, device_id_type=mesh_type)

    signal(partner)
    pl.when(has_up)(lambda: signal(r + 2))
    pl.when(has_down)(lambda: signal(r - 2))
    pl.when(has_up & has_down)(lambda: pl.semaphore_wait(barrier, 3))
    pl.when(jnp.logical_not(has_up & has_down))(lambda: pl.semaphore_wait(barrier, 2))

    for c in range(pieces):
        pl.when(has_up)(lambda: up(c).start())
        pl.when(has_down)(lambda: down(c).start())
    pair().start()
    local = pltpu.make_async_copy(own, band.at[2], own_sem)
    local.start()

    @pl.when((odd == 0) & has_up)
    def _():
        for c in range(pieces):
            down(c).wait_recv()
            passed(c).start()

    @pl.when((odd == 1) & has_down)
    def _():
        for c in range(pieces):
            up(c).wait_recv()
            passed(c).start()

    @pl.when((odd == 0) & has_down)
    def _():
        for c in range(pieces):
            up(c).wait_recv()
            passed(c).wait_recv()

    @pl.when((odd == 1) & has_up)
    def _():
        for c in range(pieces):
            down(c).wait_recv()
            passed(c).wait_recv()

    local.wait()
    pair().wait_recv()
    pair().wait_send()
    for c in range(pieces):
        pl.when(has_up)(lambda: up(c).wait_send())
        pl.when(has_down)(lambda: down(c).wait_send())

    @pl.when(((odd == 0) & has_up) | ((odd == 1) & has_down))
    def _():
        for c in range(pieces):
            passed(c).wait_send()


def gathered(p_tiles, rows):
    fine_rows = p_tiles.shape[0]
    pieces = min(8, fine_rows)
    vmem = pl.BlockSpec(memory_space=pltpu.VMEM)
    dma = pltpu.SemaphoreType.DMA
    return pl.pallas_call(
        functools.partial(gather_kernel, rows, pieces),
        out_shape=jax.ShapeDtypeStruct((5,) + p_tiles.shape, p_tiles.dtype),
        in_specs=[vmem],
        out_specs=vmem,
        scratch_shapes=[dma((2, pieces))] * 2 + [dma((2, 1)), dma((2, pieces)), dma],
        compiler_params=pltpu.CompilerParams(
            collective_id=1, has_side_effects=True, vmem_limit_bytes=16 * 1024 * 1024
        ),
    )(p_tiles)


def body(a_tiles, a_cols, p_tiles, p_cols, c_cols):
    fine_rows = a_tiles.shape[0]
    coarse_rows = fine_rows // RATIO
    tile = a_tiles.shape[-1]
    kc = c_cols.shape[1]
    chunks = lax.axis_size("grp")
    position = lax.axis_index("row")
    band = gathered(p_tiles, lax.axis_size("row"))
    band = band.reshape((5 * fine_rows,) + p_tiles.shape[1:])
    center, codes, scales = local_products(
        a_tiles, a_cols, band, p_cols, c_cols, position, chunks
    )
    out = exchange(center, codes, scales, lax.axis_size("row"))
    return out.reshape(coarse_rows, kc // chunks, tile, tile)


def solution(mesh):
    return jax.shard_map(
        body,
        mesh=mesh,
        in_specs=(
            P("row", "grp", None, None, None),
            P("row", "grp", None),
            P("row", None, None, None),
            P(),
            P(),
        ),
        out_specs=P("row", "grp", None, None),
        check_vma=False,
    )
```

profile of v0, /device:TPU:11, one launch (start us, length us, event | category | flops | bytes accessed | tf_op | source)
XLA Modules:
  0.0 105.2 jit_solution(16331809371807814281)
XLA Ops:
  0.0 0.8 copy.7
  0.8 0.6 reshape.19.a_cols
  1.4 0.8 copy.9
  2.1 0.7 reshape.21.c_cols
  2.8 0.8 copy.8
  3.6 0.7 reshape.20.p_cols
  4.2 0.0 copy-start.3
  4.2 1.2 %copy-done.3 = bf16[8,4,128,128]{3,2,1,0:T(8,128)(2,1)S(1)} copy-done((bf16[8,4,128,128]{3,2,1,0:T(8,128)(2,1)S(1)}, bf16[8,4,128,128]{3,2,1,0:T(8,128)(2,1)}, u32[]{:S(2)}) %copy-start.3) | copy-done | bytes 1048600
  5.5 28.0 %shard_map.55 = bf16[5,8,4,128,128]{4,3,2,1,0:T(8,128)(2,1)S(1)} custom-call(bf16[8,4,128,128]{3,2,1,0:T(8,128)(2,1)S(1)} %copy-done.3), custom_call_target="tpu_custom_call" | custom-call | tf_op jit(solution)/shard_map/pallas_call | solution.py:423
  33.5 0.0 copy-start
  33.5 2.3 %copy-done = bf16[5,8,4,128,128]{4,3,2,1,0:T(8,128)(2,1)} copy-done((bf16[5,8,4,128,128]{4,3,2,1,0:T(8,128)(2,1)}, bf16[5,8,4,128,128]{4,3,2,1,0:T(8,128)(2,1)S(1)}, u32[]{:S(2)}) %copy-start) | copy-done | bytes 5242904
  35.8 21.6 %shard_map.56 = (f32[4,16,128,128]{3,2,1,0:T(8,128)}, s16[2,4,16,128,128]{4,3,2,1,0:T(8,128)(2,1)}, f32[2,4,16,128]{3,2,1,0:T(8,128)}) custom-call(s32[1]{0:T(128)} %bitcast.where, s32[56]{0:T(128)} %reshape.19.a_cols, s32[256]{0:T(256)} %reshape.20.p_cols, s32[512]{0:T(512)} %reshape.21.c_cols, bf16[56,128,128]{2,1,0:T(8,128)(2,1)} %bitcast.8, ...), custom_call_target="tpu_custom_call" | custom-call | tf_op jit(solution)/shard_map/pallas_call | solution.py:116
  57.4 0.0 copy-start.1
  57.4 2.2 %copy-done.1 = f32[4,16,128,128]{3,2,1,0:T(8,128)S(1)} copy-done((f32[4,16,128,128]{3,2,1,0:T(8,128)S(1)}, f32[4,16,128,128]{3,2,1,0:T(8,128)}, u32[]{:S(2)}) %copy-start.1) | copy-done | bytes 4194328
  59.6 0.0 copy-start.2
  59.6 2.2 %copy-done.2 = s16[2,4,16,128,128]{4,3,2,1,0:T(8,128)(2,1)S(1)} copy-done((s16[2,4,16,128,128]{4,3,2,1,0:T(8,128)(2,1)S(1)}, s16[2,4,16,128,128]{4,3,2,1,0:T(8,128)(2,1)}, u32[]{:S(2)}) %copy-start.2) | copy-done | bytes 4194328
  61.7 0.0 copy-start.4
  61.7 0.8 copy-done.4
  62.6 41.6 %shard_map.57 = f32[16,128,128]{2,1,0:T(8,128)S(1)} custom-call(f32[4,16,128,128]{3,2,1,0:T(8,128)S(1)} %copy-done.1, s16[2,4,16,128,128]{4,3,2,1,0:T(8,128)(2,1)S(1)} %copy-done.2, f32[2,4,16,128]{3,2,1,0:T(8,128)S(1)} %copy-done.4), custom_call_target="tpu_custom_call" | custom-call | tf_op jit(solution)/shard_map/pallas_call | solution.py:305
  104.2 1.0 copy.11
Async XLA Ops:
  4.2 1.2 %copy-start.3 = (bf16[8,4,128,128]{3,2,1,0:T(8,128)(2,1)S(1)}, bf16[8,4,128,128]{3,2,1,0:T(8,128)(2,1)}, u32[]{:S(2)}) copy-start(bf16[8,4,128,128]{3,2,1,0:T(8,128)(2,1)} %own.1) | copy-start | bytes 3145732
  33.5 2.3 %copy-start = (bf16[5,8,4,128,128]{4,3,2,1,0:T(8,128)(2,1)}, bf16[5,8,4,128,128]{4,3,2,1,0:T(8,128)(2,1)S(1)}, u32[]{:S(2)}) copy-start(bf16[5,8,4,128,128]{4,3,2,1,0:T(8,128)(2,1)S(1)} %shard_map.55) | copy-start | bytes 15728644
  57.4 2.2 %copy-start.1 = (f32[4,16,128,128]{3,2,1,0:T(8,128)S(1)}, f32[4,16,128,128]{3,2,1,0:T(8,128)}, u32[]{:S(2)}) copy-start(f32[4,16,128,128]{3,2,1,0:T(8,128)} %get-tuple-element.8.center) | copy-start | bytes 12582916
  59.6 2.2 %copy-start.2 = (s16[2,4,16,128,128]{4,3,2,1,0:T(8,128)(2,1)S(1)}, s16[2,4,16,128,128]{4,3,2,1,0:T(8,128)(2,1)}, u32[]{:S(2)}) copy-start(s16[2,4,16,128,128]{4,3,2,1,0:T(8,128)(2,1)} %get-tuple-element.9.codes) | copy-start | bytes 12582916
  61.7 0.8 copy-start.4
where the time goes:
time: 106 us; the launch traced here: 105 us
  Pallas kernels  91.2 us (86%)
  local copies, waits for them, and re-layouts  13.9 us (13%)
    pallas_call x1, Pallas kernels, exchange(): pl.pallas_call(functools.partial(exchange_kernel, rows, chunks), out_shap...  41.6 us
    pallas_call x1, Pallas kernels, gathered(): pl.pallas_call(functools.partial(gather_kernel, rows, pieces), out_shape=...  28 us
    pallas_call x1, Pallas kernels, local_products(): pl.pallas_call(functools.partial(product_kernel, (fine_rows, slots, kp, k...  21.6 us
    unnamed x14, local copies, waits for them, and re-layouts  12 us

commit v1 on v0

--- a/solution.py
+++ b/solution.py
@@ -55,12 +55,12 @@
     def _(i):
         spread[...] = jnp.zeros_like(spread)
         for s in range(slots):
-            j = a_cols[i * slots + s]
+            j = a_cols[s, 0, i]
             local = (j - band_start) * kp
             right = jnp.concatenate([band_ref[local + p] for p in range(kp)], axis=1)
             prod = jnp.dot(a_ref[i * slots + s], right, preferred_element_type=jnp.float32)
             for p in range(kp):
-                w = p_cols[j * kp + p] - window_start
+                w = p_cols[p, j] - window_start
                 spread[w] = spread[w] + prod[:, p * tile : (p + 1) * tile]
 
         @pl.loop(0, window, unroll=4)
@@ -71,14 +71,14 @@
             halves[w, tile:] = (value - high.astype(jnp.float32)).astype(jnp.bfloat16)
 
         for q in range(kp):
-            c = p_cols[(first_row + i) * kp + q]
+            c = p_cols[q, first_row + i]
             own = band_ref[(REACH * fine_rows + i) * kp + q].T
             left = jnp.concatenate([own, own], axis=1)
             out = (c - base_coarse) * kc
             for k in range(0, kc, group):
                 parts = []
                 for n in range(group):
-                    w = c_cols[c * kc + k + n] - window_start
+                    w = c_cols[k + n, c] - window_start
                     w = jnp.where((w < 0) | (w >= window), window, w)
                     parts.append(halves[w])
                 prod = jnp.dot(
@@ -127,12 +127,12 @@
             pltpu.VMEM((window, tile, tile), jnp.float32),
             pltpu.VMEM((window + 1, 2 * tile, tile), jnp.bfloat16),
         ],
-        compiler_params=pltpu.CompilerParams(vmem_limit_bytes=56 * 1024 * 1024),
+        compiler_params=pltpu.CompilerParams(vmem_limit_bytes=34 * 1024 * 1024),
     )(
         position.reshape(1),
-        a_cols.reshape(-1),
-        p_cols.reshape(-1),
-        c_cols.reshape(-1),
+        a_cols.T,
+        p_cols.T,
+        c_cols.T,
         a_tiles.reshape(-1, tile, tile),
         band.reshape(-1, tile, tile),
     )
@@ -325,107 +325,165 @@
     )(center, codes, scales)
 
 
-def gather_kernel(rows, pieces, own, band, up_sems, down_sems, pair_sems, pass_sems, own_sem):
+def gather_kernel(
+    rows,
+    groups,
+    own,
+    band,
+    side_sems,
+    near_sems,
+    pair_sems,
+    pass_sems,
+    own_sem,
+):
     r = lax.axis_index("row")
+    g = lax.axis_index("grp")
     odd = lax.rem(r, 2)
     partner = r + 1 - 2 * odd
-    has_down = r >= 2
-    has_up = r < rows - 2
-    step = own.shape[0] // pieces
+    has = (r >= 2, r < rows - 2)
+    takes = (r < rows - 2, r >= 2)
+    blocks = (4, 0)
+    targets = (r - 2, r + 2)
+    g_odd = lax.rem(g, 2)
+    g_high = lax.rem(g // 2, 2)
+    near = (g + 1 - 2 * g_odd, g + 2 - 4 * g_high)
+    half = own.shape[0] // 2
+    parity = lax.rem(g_odd + g_high, 2)
+    mine = parity * half
+    other = (1 - parity) * half
     barrier = pltpu.get_barrier_semaphore()
     mesh_type = pl.DeviceIdType.MESH
-
-    def copy(src, dst, sems, c, to):
+    turn = half // 2
+    order = [n * turn + c for c in range(turn) for n in range(2)]
+
+    def copy(src, dst, send, recv, to):
         return pltpu.make_async_remote_copy(
             src_ref=src,
             dst_ref=dst,
-            send_sem=sems.at[0, c],
-            recv_sem=sems.at[1, c],
-            device_id={"row": to},
+            send_sem=send,
+            recv_sem=recv,
+            device_id=to,
             device_id_type=mesh_type,
         )
 
-    def part(c):
-        return pl.ds(c * step, step)
-
-    def up(c):
-        return copy(own.at[part(c)], band.at[0, part(c)], up_sems, c, r + 2)
-
-    def down(c):
-        return copy(own.at[part(c)], band.at[4, part(c)], down_sems, c, r - 2)
+    def side(d, c):
+        at = mine + c
+        return copy(
+            own.at[at],
+            band.at[blocks[d], at],
+            side_sems.at[0, d, c],
+            side_sems.at[1, d, c],
+            {"row": targets[d]},
+        )
+
+    def near_out(d, c):
+        at = mine + c
+        return copy(
+            band.at[blocks[d], at],
+            band.at[blocks[d], at],
+            near_sems.at[0, d, c],
+            near_sems.at[1, d, c],
+            {"grp": near[c // turn]},
+        )
+
+    def near_in(d, c):
+        at = other + c
+        return copy(
+            band.at[blocks[d], at],
+            band.at[blocks[d], at],
+            near_sems.at[0, d, c],
+            near_sems.at[1, d, c],
+            {"grp": near[c // turn]},
+        )
 
     def pair():
-        return copy(own, band.at[1 + 2 * odd], pair_sems, 0, partner)
-
-    def passed(c):
         return copy(
-            band.at[4 - 4 * odd, part(c)], band.at[3 - 2 * odd, part(c)], pass_sems, c, partner
+            own, band.at[1 + 2 * odd], pair_sems.at[0], pair_sems.at[1], {"row": partner}
+        )
+
+    def passed(at):
+        return copy(
+            band.at[4 - 4 * odd, at],
+            band.at[3 - 2 * odd, at],
+            pass_sems.at[0, at],
+            pass_sems.at[1, at],
+            {"row": partner},
         )
 
     def signal(to):
-        pl.semaphore_signal(barrier, inc=1, device_id={"row": to}, device_id_type=mesh_type)
-
-    signal(partner)
-    pl.when(has_up)(lambda: signal(r + 2))
-    pl.when(has_down)(lambda: signal(r - 2))
-    pl.when(has_up & has_down)(lambda: pl.semaphore_wait(barrier, 3))
-    pl.when(jnp.logical_not(has_up & has_down))(lambda: pl.semaphore_wait(barrier, 2))
-
-    for c in range(pieces):
-        pl.when(has_up)(lambda: up(c).start())
-        pl.when(has_down)(lambda: down(c).start())
+        pl.semaphore_signal(barrier, inc=1, device_id=to, device_id_type=mesh_type)
+
+    signal({"row": partner})
+    signal({"grp": near[0]})
+    signal({"grp": near[1]})
+    for d in range(2):
+        pl.when(has[d])(lambda: signal({"row": targets[d]}))
+    pl.when(has[0] & has[1])(lambda: pl.semaphore_wait(barrier, 5))
+    pl.when(jnp.logical_not(has[0] & has[1]))(lambda: pl.semaphore_wait(barrier, 4))
+
+    for c in order:
+        for d in range(2):
+            pl.when(has[d])(lambda: side(d, c).start())
     pair().start()
     local = pltpu.make_async_copy(own, band.at[2], own_sem)
     local.start()
 
-    @pl.when((odd == 0) & has_up)
+    passes = (odd == 0, odd == 1)
+
+    for c in order:
+        for d in range(2):
+
+            @pl.when(takes[d])
+            def _():
+                side(d, c).wait_recv()
+                near_out(d, c).start()
+
+            pl.when(takes[d] & passes[d])(lambda: passed(mine + c).start())
+
+    for c in order:
+        for d in range(2):
+            pl.when(takes[d])(lambda: near_in(d, c).wait_recv())
+            pl.when(takes[d] & passes[d])(lambda: passed(other + c).start())
+
+    passing = ((odd == 0) & takes[0]) | ((odd == 1) & takes[1])
+    passed_to = ((odd == 1) & takes[0]) | ((odd == 0) & takes[1])
+
+    @pl.when(passed_to)
     def _():
-        for c in range(pieces):
-            down(c).wait_recv()
-            passed(c).start()
-
-    @pl.when((odd == 1) & has_down)
-    def _():
-        for c in range(pieces):
-            up(c).wait_recv()
-            passed(c).start()
-
-    @pl.when((odd == 0) & has_down)
-    def _():
-        for c in range(pieces):
-            up(c).wait_recv()
-            passed(c).wait_recv()
-
-    @pl.when((odd == 1) & has_up)
-    def _():
-        for c in range(pieces):
-            down(c).wait_recv()
+        for c in range(2 * half):
             passed(c).wait_recv()
 
     local.wait()
     pair().wait_recv()
     pair().wait_send()
-    for c in range(pieces):
-        pl.when(has_up)(lambda: up(c).wait_send())
-        pl.when(has_down)(lambda: down(c).wait_send())
-
-    @pl.when(((odd == 0) & has_up) | ((odd == 1) & has_down))
+    for c in order:
+        for d in range(2):
+            pl.when(has[d])(lambda: side(d, c).wait_send())
+            pl.when(takes[d])(lambda: near_out(d, c).wait_send())
+
+    @pl.when(passing)
     def _():
-        for c in range(pieces):
+        for c in range(2 * half):
             passed(c).wait_send()
 
 
-def gathered(p_tiles, rows):
+def gathered(p_tiles, rows, groups):
     fine_rows = p_tiles.shape[0]
-    pieces = min(8, fine_rows)
+    half = fine_rows // 2
     vmem = pl.BlockSpec(memory_space=pltpu.VMEM)
     dma = pltpu.SemaphoreType.DMA
     return pl.pallas_call(
-        functools.partial(gather_kernel, rows, pieces),
+        functools.partial(gather_kernel, rows, groups),
         out_shape=jax.ShapeDtypeStruct((5,) + p_tiles.shape, p_tiles.dtype),
         in_specs=[vmem],
         out_specs=vmem,
-        scratch_shapes=[dma((2, pieces))] * 2 + [dma((2, 1)), dma((2, pieces)), dma],
+        scratch_shapes=[
+            dma((2, 2, half)),
+            dma((2, 2, half)),
+            dma((2,)),
+            dma((2, fine_rows)),
+            dma,
+        ],
         compiler_params=pltpu.CompilerParams(
             collective_id=1, has_side_effects=True, vmem_limit_bytes=16 * 1024 * 1024
         ),
@@ -439,7 +497,7 @@
     kc = c_cols.shape[1]
     chunks = lax.axis_size("grp")
     position = lax.axis_index("row")
-    band = gathered(p_tiles, lax.axis_size("row"))
+    band = gathered(p_tiles, lax.axis_size("row"), chunks)
     band = band.reshape((5 * fine_rows,) + p_tiles.shape[1:])
     center, codes, scales = local_products(
         a_tiles, a_cols, band, p_cols, c_cols, position, chunks

time: 106 us -> 82.1 us (0.77)
  the two profiles are of different devices: /device:TPU:11 before, /device:TPU:15 now
where the time goes in v1:
time: 82.1 us; the launch traced here: 82 us
  Pallas kernels  79.6 us (97%)
  local copies, waits for them, and re-layouts  2.35 us (3%)
    pallas_call x1, Pallas kernels, exchange(): pl.pallas_call(functools.partial(exchange_kernel, rows, chunks), out_shap...  42.1 us
    pallas_call x1, Pallas kernels, gathered(): pl.pallas_call(functools.partial(gather_kernel, rows, groups), out_shape=...  21.4 us
    pallas_call x1, Pallas kernels, local_products(): pl.pallas_call(functools.partial(product_kernel, (fine_rows, slots, kp, k...  16.1 us
    unnamed x11, local copies, waits for them, and re-layouts  2.35 us

profile of v1, /device:TPU:15, one launch (start us, length us, event | category | flops | bytes accessed | tf_op | source)
XLA Modules:
  0.0 82.0 jit_solution(14545905175097050015)
XLA Ops:
  0.0 0.0 copy-start
  0.0 0.0 copy-start.1
  0.0 1.4 %copy-done.1 = bf16[8,4,128,128]{3,2,1,0:T(8,128)(2,1)S(1)} copy-done((bf16[8,4,128,128]{3,2,1,0:T(8,128)(2,1)S(1)}, bf16[8,4,128,128]{3,2,1,0:T(8,128)(2,1)}, u32[]{:S(2)}) %copy-start.1) | copy-done | bytes 1048600
  1.4 0.0 copy-start.2
  1.4 0.0 copy-start.3
  1.4 0.0 copy-start.4
  1.4 21.4 %shard_map.55 = bf16[5,8,4,128,128]{4,3,2,1,0:T(8,128)(2,1)S(1)} custom-call(bf16[8,4,128,128]{3,2,1,0:T(8,128)(2,1)S(1)} %copy-done.1), custom_call_target="tpu_custom_call" | custom-call | tf_op jit(solution)/shard_map/pallas_call | solution.py:475
  22.8 0.0 copy-done
  22.8 0.0 copy-done.2
  22.8 0.0 copy-done.3
  22.8 0.0 copy-done.4
  22.8 16.1 %shard_map.56 = (f32[4,16,128,128]{3,2,1,0:T(8,128)S(1)}, s16[2,4,16,128,128]{4,3,2,1,0:T(8,128)(2,1)S(1)}, f32[2,4,16,128]{3,2,1,0:T(8,128)S(1)}) custom-call(s32[1]{0:T(128)} %bitcast.where, s32[7,1,8]{2,1,0:T(1,128)S(1)} %bitcast.11, s32[4,64]{1,0:T(4,128)S(1)} %bitcast.12, s32[16,32]{1,0:T(8,128)S(1)} %bitcast.10, bf16[56,128,128]{2,1,0:T(8,128)(2,1)S(1)} %bitcast.9, ...), custom_call_target="tpu_custom_call" | custom-call | tf_op jit(solution)/shard_map/pallas_call | solution.py:116
  38.9 42.1 %shard_map.57 = f32[16,128,128]{2,1,0:T(8,128)S(1)} custom-call(f32[4,16,128,128]{3,2,1,0:T(8,128)S(1)} %get-tuple-element.8.center, s16[2,4,16,128,128]{4,3,2,1,0:T(8,128)(2,1)S(1)} %get-tuple-element.9.codes, f32[2,4,16,128]{3,2,1,0:T(8,128)S(1)} %get-tuple-element.10.scales), custom_call_target="tpu_custom_call" | custom-call | tf_op jit(solution)/shard_map/pallas_call | solution.py:305
  81.0 1.0 %copy.7 = f32[4,4,128,128]{3,2,1,0:T(8,128)} copy(f32[4,4,128,128]{3,2,1,0:T(8,128)S(1)} %bitcast.8) | data formatting | bytes 2097152
Async XLA Ops:
  0.0 22.8 %copy-start = (bf16[8,1,7,128,128]{4,3,2,1,0:T(8,128)(2,1)S(1)}, bf16[8,1,7,128,128]{4,3,2,1,0:T(8,128)(2,1)}, u32[]{:S(2)}) copy-start(bf16[8,1,7,128,128]{4,3,2,1,0:T(8,128)(2,1)} %param.5) | copy-start | bytes 5505028
  0.0 1.4 %copy-start.1 = (bf16[8,4,128,128]{3,2,1,0:T(8,128)(2,1)S(1)}, bf16[8,4,128,128]{3,2,1,0:T(8,128)(2,1)}, u32[]{:S(2)}) copy-start(bf16[8,4,128,128]{3,2,1,0:T(8,128)(2,1)} %own.1) | copy-start | bytes 3145732
  1.4 21.4 %copy-start.2 = (s32[32,16]{0,1:T(8,128)S(1)}, s32[32,16]{0,1:T(8,128)}, u32[]{:S(2)}) copy-start(s32[32,16]{0,1:T(8,128)} %param.9) | copy-start | bytes 6148
  1.4 21.4 %copy-start.3 = (s32[8,1,7]{0,1,2:T(1,128)S(1)}, s32[8,1,7]{0,1,2:T(1,128)}, u32[]{:S(2)}) copy-start(s32[8,1,7]{0,1,2:T(1,128)} %param.6) | copy-start | bytes 676
  1.4 21.4 %copy-start.4 = (s32[64,4]{0,1:T(4,128)S(1)}, s32[64,4]{0,1:T(4,128)}, u32[]{:S(2)}) copy-start(s32[64,4]{0,1:T(4,128)} %param.8) | copy-start | bytes 3076

commit v2 on v1

v2 whole, which is shorter than its diff:
```python
import functools

import jax
import jax.numpy as jnp
from jax import lax
from jax.experimental import pallas as pl
from jax.experimental.pallas import tpu as pltpu
from jax.sharding import PartitionSpec as P

RATIO = 2
REACH = 2


LEVELS = 32767.0


def encoded(value):
    most = jnp.maximum(jnp.max(jnp.abs(value), axis=0, keepdims=True), 2e-34)
    code = jnp.round(value * (LEVELS / most)).astype(jnp.int32).astype(jnp.int16)
    return code, most * (1.0 / LEVELS)


def decoded(code, scale):
    return code.astype(jnp.int32).astype(jnp.float32) * scale


def product_kernel(
    sizes,
    where,
    a_cols,
    p_cols,
    a_ref,
    band_ref,
    halves,
    left_ref,
    slot_of,
    links,
    sums,
):
    fine_rows, slots, kp, tile = sizes
    coarse_rows = fine_rows // RATIO
    window = (2 * (REACH + 2) + 1) * coarse_rows
    entries = slots * kp
    empty = fine_rows * entries
    position = where[0]
    first_row = position * fine_rows
    band_start = first_row - REACH * fine_rows
    window_start = (position - REACH - 2) * coarse_rows
    base_coarse = (position - 1) * coarse_rows
    halves[empty] = jnp.zeros((2 * tile, tile), jnp.bfloat16)
    sums[entries] = jnp.zeros((tile, tile), jnp.float32)

    @pl.loop(0, fine_rows * window, unroll=8)
    def _(n):
        slot_of[n] = empty

    for c in range(3 * coarse_rows):
        links[fine_rows * kp + c] = 0

    @pl.loop(0, fine_rows)
    def _(i):
        for q in range(kp):
            left_ref[i * kp + q] = band_ref[(REACH * fine_rows + i) * kp + q].T
            e = i * kp + q
            c = fine_rows * kp + p_cols[q, first_row + i] - base_coarse
            links[e] = links[c]
            links[c] = e + 1
        for s in range(slots):
            j = a_cols[s, 0, i]
            local = (j - band_start) * kp
            right = jnp.concatenate([band_ref[local + p] for p in range(kp)], axis=1)
            prod = jnp.dot(a_ref[i * slots + s], right, preferred_element_type=jnp.float32)
            for p in range(kp):
                at = i * window + p_cols[p, j] - window_start
                before = jnp.minimum(slot_of[at] - i * entries, entries)
                now = s * kp + p
                slot_of[at] = i * entries + now
                value = sums[before] + prod[:, p * tile : (p + 1) * tile]
                sums[now] = value
                high = value.astype(jnp.bfloat16)
                halves[i * entries + now, :tile] = high
                halves[i * entries + now, tile:] = (
                    value - high.astype(jnp.float32)
                ).astype(jnp.bfloat16)


def local_products(a_tiles, a_cols, band, p_cols, position):
    fine_rows, _, slots, tile, _ = a_tiles.shape
    kp = band.shape[1]
    coarse_rows = fine_rows // RATIO
    window = (2 * (REACH + 2) + 1) * coarse_rows
    entries = slots * kp
    smem = pl.BlockSpec(memory_space=pltpu.SMEM)
    vmem = pl.BlockSpec(memory_space=pltpu.VMEM)
    return pl.pallas_call(
        functools.partial(product_kernel, (fine_rows, slots, kp, tile)),
        out_shape=[
            jax.ShapeDtypeStruct((fine_rows * entries + 1, 2 * tile, tile), jnp.bfloat16),
            jax.ShapeDtypeStruct((fine_rows * kp, tile, tile), jnp.bfloat16),
            jax.ShapeDtypeStruct((fine_rows * window,), jnp.int32),
            jax.ShapeDtypeStruct((fine_rows * kp + 3 * coarse_rows,), jnp.int32),
        ],
        in_specs=[smem] * 3 + [vmem] * 2,
        out_specs=[vmem] * 2 + [smem] * 2,
        scratch_shapes=[pltpu.VMEM((entries + 1, tile, tile), jnp.float32)],
        compiler_params=pltpu.CompilerParams(vmem_limit_bytes=28 * 1024 * 1024),
    )(
        position.reshape(1),
        a_cols.T,
        p_cols.T,
        a_tiles.reshape(-1, tile, tile),
        band.reshape(-1, tile, tile),
    )


def exchange_kernel(
    sizes,
    p_cols,
    c_cols,
    slot_of,
    links,
    halves,
    left_ref,
    out,
    runs,
    center,
    codes,
    scales,
    got_codes,
    got_scales,
    sent_codes,
    sent_scales,
    peer_codes,
    peer_scales,
    side_sems,
    side_scale_sems,
    peer_sems,
    peer_scale_sems,
):
    fine_rows, kp, kc, tile, rows, groups = sizes
    r = lax.axis_index("row")
    g = lax.axis_index("grp")
    coarse_rows = fine_rows // RATIO
    window = (2 * (REACH + 2) + 1) * coarse_rows
    window_start = (r - REACH - 2) * coarse_rows
    first_row = r * fine_rows
    share = kc // groups
    half = share // 2
    members = half * coarse_rows
    odd = lax.rem(r, 2)
    toward = 2 * odd - 1
    outer, inner = r + toward, r - toward
    has_outer = (outer >= 0) & (outer < rows)
    g_odd = lax.rem(g, 2)
    g_high = lax.rem(g // 2, 2)
    near = (g + 1 - 2 * g_odd, g + 2 - 4 * g_high)
    far = near[0] + 2 - 4 * g_high
    wanted = ((far, far), (near[0], near[1]), (near[1], near[0]), (g, g))
    steps = len(wanted)
    barrier = pltpu.get_barrier_semaphore()
    mesh_type = pl.DeviceIdType.MESH

    def signal(to):
        pl.semaphore_signal(barrier, inc=1, device_id=to, device_id_type=mesh_type)

    signal({"row": inner})
    signal({"grp": near[0]})
    signal({"grp": near[1]})
    pl.when(has_outer)(lambda: signal({"row": outer}))

    def copy(src, dst, sems, at, to):
        return pltpu.make_async_remote_copy(
            src_ref=src,
            dst_ref=dst,
            send_sem=sems.at[(0,) + at],
            recv_sem=sems.at[(1,) + at],
            device_id=to,
            device_id_type=mesh_type,
        )

    def side_copies(pos, t):
        to = {"row": inner if pos else outer}
        return (
            copy(scales.at[pos, t], got_scales.at[pos, t], side_scale_sems, (pos, t), to),
            copy(codes.at[pos, t], got_codes.at[pos, t], side_sems, (pos, t), to),
        )

    def peer_copies(n, t):
        to = {"grp": near[n]}
        return (
            copy(
                sent_scales.at[n, t], peer_scales.at[n, t], peer_scale_sems, (n, t), to
            ),
            copy(sent_codes.at[n, t], peer_codes.at[n, t], peer_sems, (n, t), to),
        )

    def start(copies):
        for one in copies:
            one.start()

    def arrive(copies):
        for one in copies:
            one.wait_recv()

    def leave(copies):
        for one in copies:
            one.wait_send()

    runs[0] = jnp.zeros(runs.shape[1:], jnp.float32)

    @pl.when(jnp.logical_not(has_outer))
    def _():
        got_scales[0] = jnp.zeros(got_scales.shape[1:], jnp.float32)

        @pl.loop(0, 2 * members)
        def _(m):
            for t in range(steps):
                got_codes[0, t, m] = jnp.zeros((tile, tile), jnp.int16)

    def compute(t):
        @pl.loop(0, fine_rows)
        def _(i):
            for q in range(kp):
                e = i * kp + q
                c = p_cols[q, first_row + i]
                own = left_ref[e]
                left = jnp.concatenate([own, own], axis=1)
                parts = []
                for n in range(share):
                    k = wanted[t][n // half] * share + n
                    w = jnp.clip(c_cols[k, c] - window_start, 0, window - 1)
                    parts.append(halves[slot_of[i * window + w]])
                prod = jnp.dot(
                    left, jnp.concatenate(parts, axis=1), preferred_element_type=jnp.float32
                )
                before = links[e]
                for n in range(share):
                    runs[e + 1, n] = runs[before, n] + prod[:, n * tile : (n + 1) * tile]

    def last(block, c):
        return links[fine_rows * kp + block * coarse_rows + c]

    def encode(t, pos):
        block = 2 * (1 - odd) if pos else 2 * odd

        @pl.loop(0, coarse_rows)
        def _(c):
            at = last(block, c)
            for n in range(share):
                m = n * coarse_rows + c
                code, scale = encoded(runs[at, n])
                codes[pos, t, m] = code
                scales[pos, t, pl.ds(m, 1)] = scale

    def keep(t):
        @pl.loop(0, coarse_rows)
        def _(c):
            at = last(1, c)
            for n in range(share):
                center[t, n * coarse_rows + c] = runs[at, n]

    def made(t):
        compute(t)
        encode(t, 0)
        if t == 0:
            pl.when(has_outer)(lambda: pl.semaphore_wait(barrier, 4))
            pl.when(jnp.logical_not(has_outer))(lambda: pl.semaphore_wait(barrier, 3))
        pl.when(has_outer)(lambda: start(side_copies(0, t)))
        encode(t, 1)
        start(side_copies(1, t))
        keep(t)

    def summed(t, m):
        value = center[t, m]
        for pos in range(2):
            value += decoded(got_codes[pos, t, m], got_scales[pos, t, pl.ds(m, 1)])
        return value

    def peer(n, t, m):
        return decoded(peer_codes[n, t, m], peer_scales[n, t, pl.ds(m, 1)])

    def come(t):
        pl.when(has_outer)(lambda: arrive(side_copies(0, t)))
        arrive(side_copies(1, t))

    def forward(t):
        come(t)
        if t == 2:
            for n in range(2):
                arrive(peer_copies(n, 0))
        for part in range(2):
            n = 1 - part if t == 2 else part

            @pl.loop(0, members)
            def _(m):
                value = summed(t, part * members + m)
                if t == 2:
                    value += peer(part, 0, m)
                code, scale = encoded(value)
                sent_codes[n, t, m] = code
                sent_scales[n, t, pl.ds(m, 1)] = scale

            start(peer_copies(n, t))

    def finish(t):
        come(t)
        for n in range(2):
            arrive(peer_copies(n, 1))
            arrive(peer_copies(n, 2))

        @pl.loop(0, coarse_rows)
        def _(c):
            for n in range(share):
                part = n // half
                m = (n - part * half) * coarse_rows + c
                value = summed(t, n * coarse_rows + c)
                out[c * share + n] = value + peer(part, 1, m) + peer(1 - part, 2, m)

    made(0)
    made(1)
    made(2)
    forward(0)
    made(3)
    forward(1)
    forward(2)
    finish(3)
    for t in range(steps):
        pl.when(has_outer)(lambda: leave(side_copies(0, t)))
        leave(side_copies(1, t))
    for t in range(steps - 1):
        for n in range(2):
            leave(peer_copies(n, t))


def exchange(halves, left, slot_of, links, p_cols, c_cols, rows, groups):
    _, tile = halves.shape[1:]
    kp = p_cols.shape[1]
    kc = c_cols.shape[1]
    fine_rows = left.shape[0] // kp
    coarse_rows = fine_rows // RATIO
    share = kc // groups
    members = share * coarse_rows
    steps = 4
    smem = pl.BlockSpec(memory_space=pltpu.SMEM)
    vmem = pl.BlockSpec(memory_space=pltpu.VMEM)
    dma = pltpu.SemaphoreType.DMA

    def tiles(*lead):
        return [
            pltpu.VMEM(lead + (tile, tile), jnp.int16),
            pltpu.VMEM(lead + (tile,), jnp.float32),
        ]

    return pl.pallas_call(
        functools.partial(exchange_kernel, (fine_rows, kp, kc, tile, rows, groups)),
        out_shape=jax.ShapeDtypeStruct((members, tile, tile), jnp.float32),
        in_specs=[smem] * 4 + [vmem] * 2,
        out_specs=vmem,
        scratch_shapes=[
            pltpu.VMEM((fine_rows * kp + 1, share, tile, tile), jnp.float32),
            pltpu.VMEM((steps, members, tile, tile), jnp.float32),
            *tiles(2, steps, members),
            *tiles(2, steps, members),
            *tiles(2, steps - 1, members // 2),
            *tiles(2, steps - 1, members // 2),
            dma((2, 2, steps)),
            dma((2, 2, steps)),
            dma((2, 2, steps - 1)),
            dma((2, 2, steps - 1)),
        ],
        compiler_params=pltpu.CompilerParams(
            collective_id=0, has_side_effects=True, vmem_limit_bytes=28 * 1024 * 1024
        ),
    )(p_cols.T, c_cols.T, slot_of, links, halves, left)


def gather_kernel(
    rows,
    groups,
    own,
    band,
    side_sems,
    near_sems,
    pair_sems,
    pass_sems,
    own_sem,
):
    r = lax.axis_index("row")
    g = lax.axis_index("grp")
    odd = lax.rem(r, 2)
    partner = r + 1 - 2 * odd
    has = (r >= 2, r < rows - 2)
    takes = (r < rows - 2, r >= 2)
    blocks = (4, 0)
    targets = (r - 2, r + 2)
    g_odd = lax.rem(g, 2)
    g_high = lax.rem(g // 2, 2)
    near = (g + 1 - 2 * g_odd, g + 2 - 4 * g_high)
    half = own.shape[0] // 2
    parity = lax.rem(g_odd + g_high, 2)
    mine = parity * half
    other = (1 - parity) * half
    barrier = pltpu.get_barrier_semaphore()
    mesh_type = pl.DeviceIdType.MESH
    turn = half // 2
    order = [n * turn + c for c in range(turn) for n in range(2)]

    def copy(src, dst, send, recv, to):
        return pltpu.make_async_remote_copy(
            src_ref=src,
            dst_ref=dst,
            send_sem=send,
            recv_sem=recv,
            device_id=to,
            device_id_type=mesh_type,
        )

    def side(d, c):
        at = mine + c
        return copy(
            own.at[at],
            band.at[blocks[d], at],
            side_sems.at[0, d, c],
            side_sems.at[1, d, c],
            {"row": targets[d]},
        )

    def near_out(d, c):
        at = mine + c
        return copy(
            band.at[blocks[d], at],
            band.at[blocks[d], at],
            near_sems.at[0, d, c],
            near_sems.at[1, d, c],
            {"grp": near[c // turn]},
        )

    def near_in(d, c):
        at = other + c
        return copy(
            band.at[blocks[d], at],
            band.at[blocks[d], at],
            near_sems.at[0, d, c],
            near_sems.at[1, d, c],
            {"grp": near[c // turn]},
        )

    def pair():
        return copy(
            own, band.at[1 + 2 * odd], pair_sems.at[0], pair_sems.at[1], {"row": partner}
        )

    def passed(at):
        return copy(
            band.at[4 - 4 * odd, at],
            band.at[3 - 2 * odd, at],
            pass_sems.at[0, at],
            pass_sems.at[1, at],
            {"row": partner},
        )

    def signal(to):
        pl.semaphore_signal(barrier, inc=1, device_id=to, device_id_type=mesh_type)

    signal({"row": partner})
    signal({"grp": near[0]})
    signal({"grp": near[1]})
    for d in range(2):
        pl.when(has[d])(lambda: signal({"row": targets[d]}))
    pl.when(has[0] & has[1])(lambda: pl.semaphore_wait(barrier, 5))
    pl.when(jnp.logical_not(has[0] & has[1]))(lambda: pl.semaphore_wait(barrier, 4))

    for c in order:
        for d in range(2):
            pl.when(has[d])(lambda: side(d, c).start())
    pair().start()
    local = pltpu.make_async_copy(own, band.at[2], own_sem)
    local.start()

    passes = (odd == 0, odd == 1)

    for c in order:
        for d in range(2):

            @pl.when(takes[d])
            def _():
                side(d, c).wait_recv()
                near_out(d, c).start()

            pl.when(takes[d] & passes[d])(lambda: passed(mine + c).start())

    for c in order:
        for d in range(2):
            pl.when(takes[d])(lambda: near_in(d, c).wait_recv())
            pl.when(takes[d] & passes[d])(lambda: passed(other + c).start())

    passing = ((odd == 0) & takes[0]) | ((odd == 1) & takes[1])
    passed_to = ((odd == 1) & takes[0]) | ((odd == 0) & takes[1])

    @pl.when(passed_to)
    def _():
        for c in range(2 * half):
            passed(c).wait_recv()

    local.wait()
    pair().wait_recv()
    pair().wait_send()
    for c in order:
        for d in range(2):
            pl.when(has[d])(lambda: side(d, c).wait_send())
            pl.when(takes[d])(lambda: near_out(d, c).wait_send())

    @pl.when(passing)
    def _():
        for c in range(2 * half):
            passed(c).wait_send()


def gathered(p_tiles, rows, groups):
    fine_rows = p_tiles.shape[0]
    half = fine_rows // 2
    vmem = pl.BlockSpec(memory_space=pltpu.VMEM)
    dma = pltpu.SemaphoreType.DMA
    return pl.pallas_call(
        functools.partial(gather_kernel, rows, groups),
        out_shape=jax.ShapeDtypeStruct((5,) + p_tiles.shape, p_tiles.dtype),
        in_specs=[vmem],
        out_specs=vmem,
        scratch_shapes=[
            dma((2, 2, half)),
            dma((2, 2, half)),
            dma((2,)),
            dma((2, fine_rows)),
            dma,
        ],
        compiler_params=pltpu.CompilerParams(
            collective_id=1, has_side_effects=True, vmem_limit_bytes=16 * 1024 * 1024
        ),
    )(p_tiles)


def body(a_tiles, a_cols, p_tiles, p_cols, c_cols):
    fine_rows = a_tiles.shape[0]
    coarse_rows = fine_rows // RATIO
    tile = a_tiles.shape[-1]
    kc = c_cols.shape[1]
    chunks = lax.axis_size("grp")
    position = lax.axis_index("row")
    band = gathered(p_tiles, lax.axis_size("row"), chunks)
    band = band.reshape((5 * fine_rows,) + p_tiles.shape[1:])
    halves, left, slot_of, links = local_products(a_tiles, a_cols, band, p_cols, position)
    out = exchange(halves, left, slot_of, links, p_cols, c_cols, lax.axis_size("row"), chunks)
    return out.reshape(coarse_rows, kc // chunks, tile, tile)


def solution(mesh):
    return jax.shard_map(
        body,
        mesh=mesh,
        in_specs=(
            P("row", "grp", None, None, None),
            P("row", "grp", None),
            P("row", None, None, None),
            P(),
            P(),
        ),
        out_specs=P("row", "grp", None, None),
        check_vma=False,
    )
```

time: 82.1 us -> 63.8 us (0.78)
  the two profiles are of different devices: /device:TPU:15 before, /device:TPU:1 now
where the time goes in v2:
time: 63.8 us; the launch traced here: 63.4 us
  Pallas kernels  60.9 us (95%)
  local copies, waits for them, and re-layouts  2.34 us (4%)
    pallas_call x1, Pallas kernels, exchange(): pl.pallas_call(functools.partial(exchange_kernel, (fine_rows, kp, kc, til...  32.4 us
    pallas_call x1, Pallas kernels, gathered(): pl.pallas_call(functools.partial(gather_kernel, rows, groups), out_shape=...  22.1 us
    pallas_call x1, Pallas kernels, local_products(): pl.pallas_call(functools.partial(product_kernel, (fine_rows, slots, kp, t...  6.44 us
    unnamed x11, local copies, waits for them, and re-layouts  2.34 us

profile of v2, /device:TPU:1, one launch (start us, length us, event | category | flops | bytes accessed | tf_op | source)
XLA Modules:
  0.0 63.4 jit_solution(16731572325436985422)
XLA Ops:
  0.0 0.0 copy-start.3
  0.0 0.0 copy-start.4
  0.0 0.0 copy-start
  0.0 0.0 copy-start.1
  0.0 1.4 %copy-done.1 = bf16[8,4,128,128]{3,2,1,0:T(8,128)(2,1)S(1)} copy-done((bf16[8,4,128,128]{3,2,1,0:T(8,128)(2,1)S(1)}, bf16[8,4,128,128]{3,2,1,0:T(8,128)(2,1)}, u32[]{:S(2)}) %copy-start.1) | copy-done | bytes 1048600
  1.4 0.0 copy-start.2
  1.4 22.1 %shard_map.55 = bf16[5,8,4,128,128]{4,3,2,1,0:T(8,128)(2,1)S(1)} custom-call(bf16[8,4,128,128]{3,2,1,0:T(8,128)(2,1)S(1)} %copy-done.1), custom_call_target="tpu_custom_call" | custom-call | tf_op jit(solution)/shard_map/pallas_call | solution.py:524
  23.4 0.0 copy-done.3
  23.4 0.0 copy-done.4
  23.5 0.0 copy-done
  23.5 6.4 %shard_map.56 = (bf16[225,256,128]{2,1,0:T(8,128)(2,1)S(1)}, bf16[32,128,128]{2,1,0:T(8,128)(2,1)S(1)}, s32[288]{0:T(512)S(1)}, s32[44]{0:T(128)S(1)}) custom-call(s32[1]{0:T(128)} %bitcast.2.where, s32[7,1,8]{2,1,0:T(1,128)S(1)} %bitcast.13, s32[4,64]{1,0:T(4,128)S(1)} %bitcast.11, bf16[56,128,128]{2,1,0:T(8,128)(2,1)S(1)} %bitcast.9, ...), custom_call_target="tpu_custom_call" | custom-call | tf_op jit(solution)/shard_map/pallas_call | solution.py:95
  29.9 0.0 copy-done.2
  29.9 32.4 %shard_map.57 = f32[16,128,128]{2,1,0:T(8,128)S(1)} custom-call(s32[4,64]{1,0:T(4,128)S(1)} %bitcast.12, s32[16,32]{1,0:T(8,128)S(1)} %bitcast.10, s32[288]{0:T(512)S(1)} %get-tuple-element.9.slot_of, s32[44]{0:T(128)S(1)} %get-tuple-element.10.links, bf16[225,256,128]{2,1,0:T(8,128)(2,1)S(1)} %get-tuple-element.11.halves, ...), custom_call_target="tpu_custom_call" | custom-call | tf_op jit(solution)/shard_map/pallas_call | solution.py:354
  62.4 1.0 %copy.7 = f32[4,4,128,128]{3,2,1,0:T(8,128)} copy(f32[4,4,128,128]{3,2,1,0:T(8,128)S(1)} %bitcast.8) | data formatting | bytes 2097152
Async XLA Ops:
  0.0 23.4 %copy-start.3 = (s32[64,4]{0,1:T(4,128)S(1)}, s32[64,4]{0,1:T(4,128)}, u32[]{:S(2)}) copy-start(s32[64,4]{0,1:T(4,128)} %param.8) | copy-start | bytes 3076
  0.0 23.4 %copy-start.4 = (s32[8,1,7]{0,1,2:T(1,128)S(1)}, s32[8,1,7]{0,1,2:T(1,128)}, u32[]{:S(2)}) copy-start(s32[8,1,7]{0,1,2:T(1,128)} %param.6) | copy-start | bytes 676
  0.0 23.5 %copy-start = (bf16[8,1,7,128,128]{4,3,2,1,0:T(8,128)(2,1)S(1)}, bf16[8,1,7,128,128]{4,3,2,1,0:T(8,128)(2,1)}, u32[]{:S(2)}) copy-start(bf16[8,1,7,128,128]{4,3,2,1,0:T(8,128)(2,1)} %param.5) | copy-start | bytes 5505028
  0.0 1.4 %copy-start.1 = (bf16[8,4,128,128]{3,2,1,0:T(8,128)(2,1)S(1)}, bf16[8,4,128,128]{3,2,1,0:T(8,128)(2,1)}, u32[]{:S(2)}) copy-start(bf16[8,4,128,128]{3,2,1,0:T(8,128)(2,1)} %own.1) | copy-start | bytes 3145732
  1.4 28.5 %copy-start.2 = (s32[32,16]{0,1:T(8,128)S(1)}, s32[32,16]{0,1:T(8,128)}, u32[]{:S(2)}) copy-start(s32[32,16]{0,1:T(8,128)} %param.9) | copy-start | bytes 6148

commit v3 on v2

--- a/solution.py
+++ b/solution.py
@@ -147,6 +147,9 @@
     share = kc // groups
     half = share // 2
     members = half * coarse_rows
+    pieces = min(fine_rows, members) // 2
+    size = members // pieces
+    pace = fine_rows // pieces
     odd = lax.rem(r, 2)
     toward = 2 * odd - 1
     outer, inner = r + toward, r - toward
@@ -178,20 +181,35 @@
             device_id_type=mesh_type,
         )
 
-    def side_copies(pos, t):
+    def side_scales(pos, t):
         to = {"row": inner if pos else outer}
-        return (
-            copy(scales.at[pos, t], got_scales.at[pos, t], side_scale_sems, (pos, t), to),
-            copy(codes.at[pos, t], got_codes.at[pos, t], side_sems, (pos, t), to),
-        )
-
-    def peer_copies(n, t):
-        to = {"grp": near[n]}
+        return (copy(scales.at[pos, t], got_scales.at[pos, t], side_scale_sems, (pos, t), to),)
+
+    def side_piece(pos, t, part, n):
+        to = {"row": inner if pos else outer}
+        some = pl.ds(part * members + n * size, size)
+        at = (pos, t, part, n)
+        return (copy(codes.at[pos, t, some], got_codes.at[pos, t, some], side_sems, at, to),)
+
+    def peer_piece(part, t, n):
+        to = {"grp": near[part]}
+        some = pl.ds(n * size, size)
+        at = (part, t, n)
         return (
             copy(
-                sent_scales.at[n, t], peer_scales.at[n, t], peer_scale_sems, (n, t), to
+                sent_scales.at[part, t, some],
+                peer_scales.at[part, t, some],
+                peer_scale_sems,
+                at,
+                to,
             ),
-            copy(sent_codes.at[n, t], peer_codes.at[n, t], peer_sems, (n, t), to),
+            copy(
+                sent_codes.at[part, t, some],
+                peer_codes.at[part, t, some],
+                peer_sems,
+                at,
+                to,
+            ),
         )
 
     def start(copies):
@@ -217,25 +235,23 @@
             for t in range(steps):
                 got_codes[0, t, m] = jnp.zeros((tile, tile), jnp.int16)
 
-    def compute(t):
-        @pl.loop(0, fine_rows)
-        def _(i):
-            for q in range(kp):
-                e = i * kp + q
-                c = p_cols[q, first_row + i]
-                own = left_ref[e]
-                left = jnp.concatenate([own, own], axis=1)
-                parts = []
-                for n in range(share):
-                    k = wanted[t][n // half] * share + n
-                    w = jnp.clip(c_cols[k, c] - window_start, 0, window - 1)
-                    parts.append(halves[slot_of[i * window + w]])
-                prod = jnp.dot(
-                    left, jnp.concatenate(parts, axis=1), preferred_element_type=jnp.float32
-                )
-                before = links[e]
-                for n in range(share):
-                    runs[e + 1, n] = runs[before, n] + prod[:, n * tile : (n + 1) * tile]
+    def compute(t, i):
+        for q in range(kp):
+            e = i * kp + q
+            c = p_cols[q, first_row + i]
+            own = left_ref[e]
+            left = jnp.concatenate([own, own], axis=1)
+            parts = []
+            for n in range(share):
+                k = wanted[t][n // half] * share + n
+                w = jnp.clip(c_cols[k, c] - window_start, 0, window - 1)
+                parts.append(halves[slot_of[i * window + w]])
+            prod = jnp.dot(
+                left, jnp.concatenate(parts, axis=1), preferred_element_type=jnp.float32
+            )
+            before = links[e]
+            for n in range(share):
+                runs[e + 1, n] = runs[before, n] + prod[:, n * tile : (n + 1) * tile]
 
     def last(block, c):
         return links[fine_rows * kp + block * coarse_rows + c]
@@ -250,7 +266,7 @@
                 m = n * coarse_rows + c
                 code, scale = encoded(runs[at, n])
                 codes[pos, t, m] = code
-                scales[pos, t, pl.ds(m, 1)] = scale
+                scales[pos, t, m] = scale
 
     def keep(t):
         @pl.loop(0, coarse_rows)
@@ -259,77 +275,102 @@
             for n in range(share):
                 center[t, n * coarse_rows + c] = runs[at, n]
 
-    def made(t):
-        compute(t)
+    def each_piece(act, pos, t):
+        for n in range(pieces):
+            for part in range(2):
+                act(side_piece(pos, t, part, n))
+
+    def send(t):
         encode(t, 0)
         if t == 0:
             pl.when(has_outer)(lambda: pl.semaphore_wait(barrier, 4))
             pl.when(jnp.logical_not(has_outer))(lambda: pl.semaphore_wait(barrier, 3))
-        pl.when(has_outer)(lambda: start(side_copies(0, t)))
+
+        @pl.when(has_outer)
+        def _():
+            start(side_scales(0, t))
+            each_piece(start, 0, t)
+
         encode(t, 1)
-        start(side_copies(1, t))
+        start(side_scales(1, t))
+        each_piece(start, 1, t)
         keep(t)
 
     def summed(t, m):
         value = center[t, m]
         for pos in range(2):
-            value += decoded(got_codes[pos, t, m], got_scales[pos, t, pl.ds(m, 1)])
+            value += decoded(got_codes[pos, t, m], got_scales[pos, t, m])
         return value
 
     def peer(n, t, m):
-        return decoded(peer_codes[n, t, m], peer_scales[n, t, pl.ds(m, 1)])
-
-    def come(t):
-        pl.when(has_outer)(lambda: arrive(side_copies(0, t)))
-        arrive(side_copies(1, t))
-
-    def forward(t):
-        come(t)
-        if t == 2:
-            for n in range(2):
-                arrive(peer_copies(n, 0))
+        return decoded(peer_codes[n, t, m], peer_scales[n, t, m])
+
+    def open_step(t):
+        pl.when(has_outer)(lambda: arrive(side_scales(0, t)))
+        arrive(side_scales(1, t))
+
+    def come(t, part, n):
+        pl.when(has_outer)(lambda: arrive(side_piece(0, t, part, n)))
+        arrive(side_piece(1, t, part, n))
+
+    def forward(t, n):
         for part in range(2):
-            n = 1 - part if t == 2 else part
-
-            @pl.loop(0, members)
-            def _(m):
+            to = 1 - part if t == 2 else part
+            come(t, part, n)
+            if t == 2:
+                arrive(peer_piece(part, 0, n))
+            for u in range(size):
+                m = n * size + u
                 value = summed(t, part * members + m)
                 if t == 2:
                     value += peer(part, 0, m)
                 code, scale = encoded(value)
-                sent_codes[n, t, m] = code
-                sent_scales[n, t, pl.ds(m, 1)] = scale
-
-            start(peer_copies(n, t))
-
-    def finish(t):
-        come(t)
-        for n in range(2):
-            arrive(peer_copies(n, 1))
-            arrive(peer_copies(n, 2))
-
-        @pl.loop(0, coarse_rows)
-        def _(c):
-            for n in range(share):
-                part = n // half
-                m = (n - part * half) * coarse_rows + c
-                value = summed(t, n * coarse_rows + c)
-                out[c * share + n] = value + peer(part, 1, m) + peer(1 - part, 2, m)
-
-    made(0)
-    made(1)
-    made(2)
-    forward(0)
-    made(3)
-    forward(1)
-    forward(2)
-    finish(3)
+                sent_codes[to, t, m] = code
+                sent_scales[to, t, m] = scale
+            start(peer_piece(to, t, n))
+
+    def finish(t, n):
+        for part in range(2):
+            come(t, part, n)
+            arrive(peer_piece(part, 1, n))
+            arrive(peer_piece(1 - part, 2, n))
+            for u in range(size):
+                m = n * size + u
+                c = lax.rem(m, coarse_rows)
+                k = part * half + m // coarse_rows
+                value = summed(t, part * members + m)
+                out[c * share + k] = value + peer(part, 1, m) + peer(1 - part, 2, m)
+
+    for t in range(2):
+        pl.loop(0, fine_rows)(lambda i: compute(t, i))
+        send(t)
+    for t in range(2):
+        open_step(t)
+
+        @pl.loop(0, pieces)
+        def _(n):
+            for u in range(pace):
+                compute(t + 2, n * pace + u)
+            forward(t, n)
+
+        send(t + 2)
+    open_step(2)
+    pl.loop(0, pieces)(lambda n: forward(2, n))
+    open_step(3)
+    pl.loop(0, pieces)(lambda n: finish(3, n))
     for t in range(steps):
-        pl.when(has_outer)(lambda: leave(side_copies(0, t)))
-        leave(side_copies(1, t))
+
+        @pl.when(has_outer)
+        def _():
+            leave(side_scales(0, t))
+            each_piece(leave, 0, t)
+
+        leave(side_scales(1, t))
+        each_piece(leave, 1, t)
     for t in range(steps - 1):
-        for n in range(2):
-            leave(peer_copies(n, t))
+        for part in range(2):
+            for n in range(pieces):
+                leave(peer_piece(part, t, n))
 
 
 def exchange(halves, left, slot_of, links, p_cols, c_cols, rows, groups):
@@ -340,6 +381,7 @@
     coarse_rows = fine_rows // RATIO
     share = kc // groups
     members = share * coarse_rows
+    pieces = min(fine_rows, members // 2) // 2
     steps = 4
     smem = pl.BlockSpec(memory_space=pltpu.SMEM)
     vmem = pl.BlockSpec(memory_space=pltpu.VMEM)
@@ -348,7 +390,7 @@
     def tiles(*lead):
         return [
             pltpu.VMEM(lead + (tile, tile), jnp.int16),
-            pltpu.VMEM(lead + (tile,), jnp.float32),
+            pltpu.VMEM(lead + (1, tile), jnp.float32),
         ]
 
     return pl.pallas_call(
@@ -363,10 +405,10 @@
             *tiles(2, steps, members),
             *tiles(2, steps - 1, members // 2),
             *tiles(2, steps - 1, members // 2),
+            dma((2, 2, steps, 2, pieces)),
             dma((2, 2, steps)),
-            dma((2, 2, steps)),
-            dma((2, 2, steps - 1)),
-            dma((2, 2, steps - 1)),
+            dma((2, 2, steps - 1, pieces)),
+            dma((2, 2, steps - 1, pieces)),
         ],
         compiler_params=pltpu.CompilerParams(
             collective_id=0, has_side_effects=True, vmem_limit_bytes=28 * 1024 * 1024
@@ -376,11 +418,13 @@
 
 def gather_kernel(
     rows,
-    groups,
+    passing,
     own,
     band,
-    side_sems,
-    near_sems,
+    side_sends,
+    side_comes,
+    near_sends,
+    near_comes,
     pair_sems,
     pass_sems,
     own_sem,
@@ -390,20 +434,21 @@
     odd = lax.rem(r, 2)
     partner = r + 1 - 2 * odd
     has = (r >= 2, r < rows - 2)
-    takes = (r < rows - 2, r >= 2)
-    blocks = (4, 0)
-    targets = (r - 2, r + 2)
+    handed, kept = odd, 1 - odd
+    takes_handed = jnp.where(odd == 0, r < rows - 2, r >= 2)
+    takes_kept = jnp.where(odd == 0, r >= 2, r < rows - 2)
     g_odd = lax.rem(g, 2)
     g_high = lax.rem(g // 2, 2)
     near = (g + 1 - 2 * g_odd, g + 2 - 4 * g_high)
-    half = own.shape[0] // 2
     parity = lax.rem(g_odd + g_high, 2)
-    mine = parity * half
-    other = (1 - parity) * half
+    tiles = own.shape[0]
+    direct = tiles - passing
+    mine = parity * direct
+    other = (1 - parity) * direct
     barrier = pltpu.get_barrier_semaphore()
     mesh_type = pl.DeviceIdType.MESH
-    turn = half // 2
-    order = [n * turn + c for c in range(turn) for n in range(2)]
+    local = pltpu.make_async_copy(own, band.at[2], own_sem)
+    local.start()
 
     def copy(src, dst, send, recv, to):
         return pltpu.make_async_remote_copy(
@@ -415,47 +460,40 @@
             device_id_type=mesh_type,
         )
 
-    def side(d, c):
-        at = mine + c
+    def place(n):
+        return mine + n if n < passing else n
+
+    def side(d, at, size, n):
+        part = pl.ds(at, size)
         return copy(
-            own.at[at],
-            band.at[blocks[d], at],
-            side_sems.at[0, d, c],
-            side_sems.at[1, d, c],
-            {"row": targets[d]},
+            band.at[2, part],
+            band.at[4 - 4 * d, part],
+            side_sends.at[d],
+            side_comes.at[d, n],
+            {"row": r - 2 + 4 * d},
         )
 
-    def near_out(d, c):
-        at = mine + c
-        return copy(
-            band.at[blocks[d], at],
-            band.at[blocks[d], at],
-            near_sems.at[0, d, c],
-            near_sems.at[1, d, c],
-            {"grp": near[c // turn]},
-        )
-
-    def near_in(d, c):
-        at = other + c
-        return copy(
-            band.at[blocks[d], at],
-            band.at[blocks[d], at],
-            near_sems.at[0, d, c],
-            near_sems.at[1, d, c],
-            {"grp": near[c // turn]},
-        )
+    def near_copy(d, at, size, n):
+        ref = band.at[4 - 4 * d, pl.ds(at, size)]
+        to = {"grp": near[n % 2]}
+        return copy(ref, ref, near_sends.at[d], near_comes.at[d, n], to)
 
     def pair():
         return copy(
-            own, band.at[1 + 2 * odd], pair_sems.at[0], pair_sems.at[1], {"row": partner}
+            band.at[2],
+            band.at[1 + 2 * odd],
+            pair_sems.at[0],
+            pair_sems.at[1],
+            {"row": partner},
         )
 
-    def passed(at):
+    def passed(at, size):
+        part = pl.ds(at, size)
         return copy(
-            band.at[4 - 4 * odd, at],
-            band.at[3 - 2 * odd, at],
-            pass_sems.at[0, at],
-            pass_sems.at[1, at],
+            band.at[4 - 4 * odd, part],
+            band.at[3 - 2 * odd, part],
+            pass_sems.at[0],
+            pass_sems.at[1],
             {"row": partner},
         )
 
@@ -466,77 +504,86 @@
     signal({"grp": near[0]})
     signal({"grp": near[1]})
     for d in range(2):
-        pl.when(has[d])(lambda: signal({"row": targets[d]}))
+        pl.when(has[d])(lambda: signal({"row": r - 2 + 4 * d}))
+    local.wait()
     pl.when(has[0] & has[1])(lambda: pl.semaphore_wait(barrier, 5))
     pl.when(jnp.logical_not(has[0] & has[1]))(lambda: pl.semaphore_wait(barrier, 4))
 
-    for c in order:
-        for d in range(2):
-            pl.when(has[d])(lambda: side(d, c).start())
+    for d in range(2):
+
+        @pl.when(has[d])
+        def _():
+            for n in range(direct):
+                side(d, place(n), 1, n).start()
+
     pair().start()
-    local = pltpu.make_async_copy(own, band.at[2], own_sem)
-    local.start()
-
-    passes = (odd == 0, odd == 1)
-
-    for c in order:
-        for d in range(2):
-
-            @pl.when(takes[d])
+
+    for n in range(direct):
+
+        @pl.when(takes_handed)
+        def _():
+            side(handed, place(n), 1, n).wait_recv()
+            if n < passing:
+                near_copy(handed, mine + n, 1, n).start()
+            passed(place(n), 1).start()
+
+        if n < passing:
+
+            @pl.when(takes_kept)
             def _():
-                side(d, c).wait_recv()
-                near_out(d, c).start()
-
-            pl.when(takes[d] & passes[d])(lambda: passed(mine + c).start())
-
-    for c in order:
-        for d in range(2):
-            pl.when(takes[d])(lambda: near_in(d, c).wait_recv())
-            pl.when(takes[d] & passes[d])(lambda: passed(other + c).start())
-
-    passing = ((odd == 0) & takes[0]) | ((odd == 1) & takes[1])
-    passed_to = ((odd == 1) & takes[0]) | ((odd == 0) & takes[1])
-
-    @pl.when(passed_to)
+                side(kept, place(n), 1, n).wait_recv()
+                near_copy(kept, mine + n, 1, n).start()
+
+    @pl.when(takes_handed)
     def _():
-        for c in range(2 * half):
-            passed(c).wait_recv()
-
-    local.wait()
+        for n in range(passing):
+            near_copy(handed, other + n, 1, n).wait_recv()
+            passed(other + n, 1).start()
+
+    @pl.when(takes_kept)
+    def _():
+        for n in range(passing, direct):
+            side(kept, place(n), 1, n).wait_recv()
+        for n in range(passing):
+            near_copy(kept, other + n, 1, n).wait_recv()
+        passed(0, tiles).wait_recv()
+        near_copy(kept, mine, passing, 0).wait_send()
+
     pair().wait_recv()
     pair().wait_send()
-    for c in order:
-        for d in range(2):
-            pl.when(has[d])(lambda: side(d, c).wait_send())
-            pl.when(takes[d])(lambda: near_out(d, c).wait_send())
-
-    @pl.when(passing)
+    for d in range(2):
+        pl.when(has[d])(lambda: side(d, 0, direct, 0).wait_send())
+
+    @pl.when(takes_handed)
     def _():
-        for c in range(2 * half):
-            passed(c).wait_send()
-
-
-def gathered(p_tiles, rows, groups):
-    fine_rows = p_tiles.shape[0]
-    half = fine_rows // 2
-    vmem = pl.BlockSpec(memory_space=pltpu.VMEM)
+        near_copy(handed, mine, passing, 0).wait_send()
+        passed(0, tiles).wait_send()
+
+
+def gathered(p_tiles, rows):
+    tile = p_tiles.shape[-1]
+    own = p_tiles.reshape(-1, tile, tile)
+    tiles = own.shape[0]
+    passing = tiles * 7 // 32 * 2
     dma = pltpu.SemaphoreType.DMA
     return pl.pallas_call(
-        functools.partial(gather_kernel, rows, groups),
-        out_shape=jax.ShapeDtypeStruct((5,) + p_tiles.shape, p_tiles.dtype),
-        in_specs=[vmem],
-        out_specs=vmem,
+        functools.partial(gather_kernel, rows, passing),
+        out_shape=jax.ShapeDtypeStruct((5,) + own.shape, own.dtype),
+        in_specs=[pl.BlockSpec(memory_space=pltpu.HBM)],
+        out_specs=pl.BlockSpec(memory_space=pltpu.VMEM),
         scratch_shapes=[
-            dma((2, 2, half)),
-            dma((2, 2, half)),
             dma((2,)),
-            dma((2, fine_rows)),
+            dma((2, tiles - passing)),
+            dma((2,)),
+            dma((2, passing)),
+            dma((2,)),
+            dma((2,)),
             dma,
         ],
         compiler_params=pltpu.CompilerParams(
             collective_id=1, has_side_effects=True, vmem_limit_bytes=16 * 1024 * 1024
         ),
-    )(p_tiles)
+    )(own)
 
 
 def body(a_tiles, a_cols, p_tiles, p_cols, c_cols):
@@ -546,7 +593,7 @@
     kc = c_cols.shape[1]
     chunks = lax.axis_size("grp")
     position = lax.axis_index("row")
-    band = gathered(p_tiles, lax.axis_size("row"), chunks)
+    band = gathered(p_tiles, lax.axis_size("row"))
     band = band.reshape((5 * fine_rows,) + p_tiles.shape[1:])
     halves, left, slot_of, links = local_products(a_tiles, a_cols, band, p_cols, position)
     out = exchange(halves, left, slot_of, links, p_cols, c_cols, lax.axis_size("row"), chunks)

time: 63.8 us -> 61.5 us (0.964)
  Pallas kernels: 60.9 us -> 59 us
    pallas_call x1, Pallas kernels: 22.1 us -> 20.9 us  [gathered(): pl.pallas_call(functools.partial(gather_kernel, rows, passing), out_shape...]
    pallas_call x1, Pallas kernels: 32.4 us -> 31.7 us  [exchange(): pl.pallas_call(functools.partial(exchange_kernel, (fine_rows, kp, kc, til...]
where the time goes in v3:
time: 61.5 us; the launch traced here: 61.4 us
  Pallas kernels  59 us (96%)
  local copies, waits for them, and re-layouts  2.34 us (4%)
    pallas_call x1, Pallas kernels, exchange(): pl.pallas_call(functools.partial(exchange_kernel, (fine_rows, kp, kc, til...  31.7 us
    pallas_call x1, Pallas kernels, gathered(): pl.pallas_call(functools.partial(gather_kernel, rows, passing), out_shape...  20.9 us
    pallas_call x1, Pallas kernels, local_products(): pl.pallas_call(functools.partial(product_kernel, (fine_rows, slots, kp, t...  6.44 us
    unnamed x11, local copies, waits for them, and re-layouts  2.34 us

profile of v3, /device:TPU:1, one launch (start us, length us, event | category | flops | bytes accessed | tf_op | source)
XLA Modules:
  0.0 61.4 jit_solution(4223177193801905022)
XLA Ops:
  0.0 0.0 copy-start.3
  0.0 0.0 copy-start.4
  0.0 0.0 copy-start
  0.0 0.0 copy-start.1
  0.0 1.4 %copy-done.1 = bf16[8,4,128,128]{3,2,1,0:T(8,128)(2,1)S(1)} copy-done((bf16[8,4,128,128]{3,2,1,0:T(8,128)(2,1)S(1)}, bf16[8,4,128,128]{3,2,1,0:T(8,128)(2,1)}, u32[]{:S(2)}) %copy-start.1) | copy-done | bytes 1048600
  1.4 0.0 copy-start.2
  1.4 20.9 %shard_map.55 = bf16[5,32,128,128]{3,2,1,0:T(8,128)(2,1)S(1)} custom-call(bf16[32,128,128]{2,1,0:T(8,128)(2,1)S(1)} %bitcast.11), custom_call_target="tpu_custom_call" | custom-call | tf_op jit(solution)/shard_map/pallas_call | solution.py:569
  22.2 0.0 copy-done.3
  22.3 0.0 copy-done.4
  22.3 0.0 copy-done
  22.3 6.4 %shard_map.56 = (bf16[225,256,128]{2,1,0:T(8,128)(2,1)S(1)}, bf16[32,128,128]{2,1,0:T(8,128)(2,1)S(1)}, s32[288]{0:T(512)S(1)}, s32[44]{0:T(128)S(1)}) custom-call(s32[1]{0:T(128)} %bitcast.2.where, s32[7,1,8]{2,1,0:T(1,128)S(1)} %bitcast.15, s32[4,64]{1,0:T(4,128)S(1)} %bitcast.13, bf16[56,128,128]{2,1,0:T(8,128)(2,1)S(1)} %bitcast.10, ...), custom_call_target="tpu_custom_call" | custom-call | tf_op jit(solution)/shard_map/pallas_call | solution.py:95
  28.7 0.0 copy-done.2
  28.7 31.7 %shard_map.57 = f32[16,128,128]{2,1,0:T(8,128)S(1)} custom-call(s32[4,64]{1,0:T(4,128)S(1)} %bitcast.14, s32[16,32]{1,0:T(8,128)S(1)} %bitcast.12, s32[288]{0:T(512)S(1)} %get-tuple-element.9.slot_of, s32[44]{0:T(128)S(1)} %get-tuple-element.10.links, bf16[225,256,128]{2,1,0:T(8,128)(2,1)S(1)} %get-tuple-element.11.halves, ...), custom_call_target="tpu_custom_call" | custom-call | tf_op jit(solution)/shard_map/pallas_call | solution.py:396
  60.4 1.0 %copy.7 = f32[4,4,128,128]{3,2,1,0:T(8,128)} copy(f32[4,4,128,128]{3,2,1,0:T(8,128)S(1)} %bitcast.9) | data formatting | bytes 2097152
Async XLA Ops:
  0.0 22.3 %copy-start.3 = (s32[64,4]{0,1:T(4,128)S(1)}, s32[64,4]{0,1:T(4,128)}, u32[]{:S(2)}) copy-start(s32[64,4]{0,1:T(4,128)} %param.8) | copy-start | bytes 3076
  0.0 22.3 %copy-start.4 = (s32[8,1,7]{0,1,2:T(1,128)S(1)}, s32[8,1,7]{0,1,2:T(1,128)}, u32[]{:S(2)}) copy-start(s32[8,1,7]{0,1,2:T(1,128)} %param.6) | copy-start | bytes 676
  0.0 22.3 %copy-start = (bf16[8,1,7,128,128]{4,3,2,1,0:T(8,128)(2,1)S(1)}, bf16[8,1,7,128,128]{4,3,2,1,0:T(8,128)(2,1)}, u32[]{:S(2)}) copy-start(bf16[8,1,7,128,128]{4,3,2,1,0:T(8,128)(2,1)} %param.5) | copy-start | bytes 5505028
  0.0 1.4 %copy-start.1 = (bf16[8,4,128,128]{3,2,1,0:T(8,128)(2,1)S(1)}, bf16[8,4,128,128]{3,2,1,0:T(8,128)(2,1)}, u32[]{:S(2)}) copy-start(bf16[8,4,128,128]{3,2,1,0:T(8,128)(2,1)} %param.7) | copy-start | bytes 3145732
  1.4 27.4 %copy-start.2 = (s32[32,16]{0,1:T(8,128)S(1)}, s32[32,16]{0,1:T(8,128)}, u32[]{:S(2)}) copy-start(s32[32,16]{0,1:T(8,128)} %param.9) | copy-start | bytes 6148

commit v4 on v3

--- a/solution.py
+++ b/solution.py
@@ -50,15 +50,13 @@
     halves[empty] = jnp.zeros((2 * tile, tile), jnp.bfloat16)
     sums[entries] = jnp.zeros((tile, tile), jnp.float32)
 
-    @pl.loop(0, fine_rows * window, unroll=8)
-    def _(n):
-        slot_of[n] = empty
-
     for c in range(3 * coarse_rows):
         links[fine_rows * kp + c] = 0
 
-    @pl.loop(0, fine_rows)
+    @pl.loop(0, fine_rows, unroll=4)
     def _(i):
+        for w in range(window):
+            slot_of[i * window + w] = empty
         for q in range(kp):
             left_ref[i * kp + q] = band_ref[(REACH * fine_rows + i) * kp + q].T
             e = i * kp + q
@@ -132,10 +130,14 @@
     sent_scales,
     peer_codes,
     peer_scales,
+    hop_codes,
+    hop_scales,
     side_sems,
     side_scale_sems,
     peer_sems,
     peer_scale_sems,
+    hop_sems,
+    hop_scale_sems,
 ):
     fine_rows, kp, kc, tile, rows, groups = sizes
     r = lax.axis_index("row")
@@ -150,6 +152,8 @@
     pieces = min(fine_rows, members) // 2
     size = members // pieces
     pace = fine_rows // pieces
+    bent = half // 2
+    turned = bent * coarse_rows // size
     odd = lax.rem(r, 2)
     toward = 2 * odd - 1
     outer, inner = r + toward, r - toward
@@ -190,6 +194,14 @@
         some = pl.ds(part * members + n * size, size)
         at = (pos, t, part, n)
         return (copy(codes.at[pos, t, some], got_codes.at[pos, t, some], side_sems, at, to),)
+
+    def hop_copies(part):
+        to = {"grp": near[part]}
+        some = pl.ds(part * members, turned * size)
+        return (
+            copy(scales.at[0, 0, some], hop_scales.at[part], hop_scale_sems, (part,), to),
+            copy(codes.at[0, 0, some], hop_codes.at[part], hop_sems, (part,), to),
+        )
 
     def peer_piece(part, t, n):
         to = {"grp": near[part]}
@@ -264,7 +276,13 @@
             at = last(block, c)
             for n in range(share):
                 m = n * coarse_rows + c
-                code, scale = encoded(runs[at, n])
+                value = runs[at, n]
+                if t == 2 and pos == 0 and n % half < bent:
+                    at_hop = n % half * coarse_rows + c
+                    value += decoded(
+                        hop_codes[n // half, at_hop], hop_scales[n // half, at_hop]
+                    )
+                code, scale = encoded(value)
                 codes[pos, t, m] = code
                 scales[pos, t, m] = scale
 
@@ -276,12 +294,18 @@
                 center[t, n * coarse_rows + c] = runs[at, n]
 
     def each_piece(act, pos, t):
-        for n in range(pieces):
+        for n in range(0 if t or pos else turned, pieces):
             for part in range(2):
                 act(side_piece(pos, t, part, n))
 
     def send(t):
-        encode(t, 0)
+        @pl.when(has_outer)
+        def _():
+            if t == 2:
+                for part in range(2):
+                    arrive(hop_copies(part))
+            encode(t, 0)
+
         if t == 0:
             pl.when(has_outer)(lambda: pl.semaphore_wait(barrier, 4))
             pl.when(jnp.logical_not(has_outer))(lambda: pl.semaphore_wait(barrier, 3))
@@ -290,38 +314,44 @@
         def _():
             start(side_scales(0, t))
             each_piece(start, 0, t)
+            if t == 0:
+                for part in range(2):
+                    start(hop_copies(part))
 
         encode(t, 1)
         start(side_scales(1, t))
         each_piece(start, 1, t)
         keep(t)
 
-    def summed(t, m):
+    def summed(t, m, skip=0):
         value = center[t, m]
-        for pos in range(2):
+        for pos in range(skip, 2):
             value += decoded(got_codes[pos, t, m], got_scales[pos, t, m])
         return value
 
     def peer(n, t, m):
         return decoded(peer_codes[n, t, m], peer_scales[n, t, m])
 
-    def open_step(t):
-        pl.when(has_outer)(lambda: arrive(side_scales(0, t)))
-        arrive(side_scales(1, t))
-
-    def come(t, part, n):
-        pl.when(has_outer)(lambda: arrive(side_piece(0, t, part, n)))
+    def open_step(t, pos):
+        if pos:
+            arrive(side_scales(1, t))
+        else:
+            pl.when(has_outer)(lambda: arrive(side_scales(0, t)))
+
+    def come(t, part, n, skip=0):
+        if not skip:
+            pl.when(has_outer)(lambda: arrive(side_piece(0, t, part, n)))
         arrive(side_piece(1, t, part, n))
 
-    def forward(t, n):
+    def forward(t, n, skip=0):
         for part in range(2):
             to = 1 - part if t == 2 else part
-            come(t, part, n)
+            come(t, part, n, skip)
             if t == 2:
                 arrive(peer_piece(part, 0, n))
             for u in range(size):
                 m = n * size + u
-                value = summed(t, part * members + m)
+                value = summed(t, part * members + m, skip)
                 if t == 2:
                     value += peer(part, 0, m)
                 code, scale = encoded(value)
@@ -341,22 +371,43 @@
                 value = summed(t, part * members + m)
                 out[c * share + k] = value + peer(part, 1, m) + peer(1 - part, 2, m)
 
-    for t in range(2):
-        pl.loop(0, fine_rows)(lambda i: compute(t, i))
-        send(t)
-    for t in range(2):
-        open_step(t)
-
-        @pl.loop(0, pieces)
-        def _(n):
-            for u in range(pace):
-                compute(t + 2, n * pace + u)
-            forward(t, n)
-
-        send(t + 2)
-    open_step(2)
+    pl.loop(0, fine_rows, unroll=4)(lambda i: compute(0, i))
+    send(0)
+    open_step(0, 1)
+
+    @pl.loop(0, turned)
+    def _(n):
+        for u in range(pace):
+            compute(1, n * pace + u)
+        forward(0, n, 1)
+
+    pl.loop(turned * pace, fine_rows, unroll=4)(lambda i: compute(1, i))
+    send(1)
+    open_step(0, 0)
+    quick = fine_rows // (pieces - turned)
+
+    @pl.loop(turned, pieces)
+    def _(n):
+        forward(0, n)
+        for u in range(quick):
+            compute(2, (n - turned) * quick + u)
+
+    send(2)
+    open_step(1, 1)
+    open_step(1, 0)
+
+    @pl.loop(0, pieces)
+    def _(n):
+        forward(1, n)
+        for u in range(pace):
+            compute(3, n * pace + u)
+
+    send(3)
+    open_step(2, 1)
+    open_step(2, 0)
     pl.loop(0, pieces)(lambda n: forward(2, n))
-    open_step(3)
+    open_step(3, 1)
+    open_step(3, 0)
     pl.loop(0, pieces)(lambda n: finish(3, n))
     for t in range(steps):
 
@@ -364,6 +415,9 @@
         def _():
             leave(side_scales(0, t))
             each_piece(leave, 0, t)
+            if t == 0:
+                for part in range(2):
+                    leave(hop_copies(part))
 
         leave(side_scales(1, t))
         each_piece(leave, 1, t)
@@ -405,10 +459,13 @@
             *tiles(2, steps, members),
             *tiles(2, steps - 1, members // 2),
             *tiles(2, steps - 1, members // 2),
+            *tiles(2, share // 4 * coarse_rows),
             dma((2, 2, steps, 2, pieces)),
             dma((2, 2, steps)),
             dma((2, 2, steps - 1, pieces)),
             dma((2, 2, steps - 1, pieces)),
+            dma((2, 2)),
+            dma((2, 2)),
         ],
         compiler_params=pltpu.CompilerParams(
             collective_id=0, has_side_effects=True, vmem_limit_bytes=28 * 1024 * 1024

time: 61.5 us -> 58.4 us (0.950)
  Pallas kernels: 59 us -> 55.8 us
    pallas_call x1, Pallas kernels: 31.7 us -> 29.2 us  [exchange(): pl.pallas_call(functools.partial(exchange_kernel, (fine_rows, kp, kc, til...]
    pallas_call x1, Pallas kernels: 6.44 us -> 5.76 us  [local_products(): pl.pallas_call(functools.partial(product_kernel, (fine_rows, slots, kp, t...]
where the time goes in v4:
time: 58.4 us; the launch traced here: 58.3 us
  Pallas kernels  55.8 us (96%)
  local copies, waits for them, and re-layouts  2.34 us (4%)
    pallas_call x1, Pallas kernels, exchange(): pl.pallas_call(functools.partial(exchange_kernel, (fine_rows, kp, kc, til...  29.2 us
    pallas_call x1, Pallas kernels, gathered(): pl.pallas_call(functools.partial(gather_kernel, rows, passing), out_shape...  20.9 us
    pallas_call x1, Pallas kernels, local_products(): pl.pallas_call(functools.partial(product_kernel, (fine_rows, slots, kp, t...  5.76 us
    unnamed x11, local copies, waits for them, and re-layouts  2.34 us

profile of v4, /device:TPU:1, one launch (start us, length us, event | category | flops | bytes accessed | tf_op | source)
XLA Modules:
  0.0 58.3 jit_solution(10117065908887770614)
XLA Ops:
  0.0 0.0 copy-start.3
  0.0 0.0 copy-start.4
  0.0 0.0 copy-start
  0.0 0.0 copy-start.1
  0.0 1.4 %copy-done.1 = bf16[8,4,128,128]{3,2,1,0:T(8,128)(2,1)S(1)} copy-done((bf16[8,4,128,128]{3,2,1,0:T(8,128)(2,1)S(1)}, bf16[8,4,128,128]{3,2,1,0:T(8,128)(2,1)}, u32[]{:S(2)}) %copy-start.1) | copy-done | bytes 1048600
  1.4 0.0 copy-start.2
  1.4 20.9 %shard_map.55 = bf16[5,32,128,128]{3,2,1,0:T(8,128)(2,1)S(1)} custom-call(bf16[32,128,128]{2,1,0:T(8,128)(2,1)S(1)} %bitcast.11), custom_call_target="tpu_custom_call" | custom-call | tf_op jit(solution)/shard_map/pallas_call | solution.py:626
  22.2 0.0 copy-done.3
  22.3 0.0 copy-done.4
  22.3 0.0 copy-done
  22.3 5.8 %shard_map.56 = (bf16[225,256,128]{2,1,0:T(8,128)(2,1)S(1)}, bf16[32,128,128]{2,1,0:T(8,128)(2,1)S(1)}, s32[288]{0:T(512)S(1)}, s32[44]{0:T(128)S(1)}) custom-call(s32[1]{0:T(128)} %bitcast.2.where, s32[7,1,8]{2,1,0:T(1,128)S(1)} %bitcast.15, s32[4,64]{1,0:T(4,128)S(1)} %bitcast.13, bf16[56,128,128]{2,1,0:T(8,128)(2,1)S(1)} %bitcast.10, ...), custom_call_target="tpu_custom_call" | custom-call | tf_op jit(solution)/shard_map/pallas_call | solution.py:93
  28.0 0.0 copy-done.2
  28.1 29.2 %shard_map.57 = f32[16,128,128]{2,1,0:T(8,128)S(1)} custom-call(s32[4,64]{1,0:T(4,128)S(1)} %bitcast.14, s32[16,32]{1,0:T(8,128)S(1)} %bitcast.12, s32[288]{0:T(512)S(1)} %get-tuple-element.9.slot_of, s32[44]{0:T(128)S(1)} %get-tuple-element.10.links, bf16[225,256,128]{2,1,0:T(8,128)(2,1)S(1)} %get-tuple-element.11.halves, ...), custom_call_target="tpu_custom_call" | custom-call | tf_op jit(solution)/shard_map/pallas_call | solution.py:450
  57.3 1.0 %copy.7 = f32[4,4,128,128]{3,2,1,0:T(8,128)} copy(f32[4,4,128,128]{3,2,1,0:T(8,128)S(1)} %bitcast.9) | data formatting | bytes 2097152
Async XLA Ops:
  0.0 22.3 %copy-start.3 = (s32[64,4]{0,1:T(4,128)S(1)}, s32[64,4]{0,1:T(4,128)}, u32[]{:S(2)}) copy-start(s32[64,4]{0,1:T(4,128)} %param.8) | copy-start | bytes 3076
  0.0 22.3 %copy-start.4 = (s32[8,1,7]{0,1,2:T(1,128)S(1)}, s32[8,1,7]{0,1,2:T(1,128)}, u32[]{:S(2)}) copy-start(s32[8,1,7]{0,1,2:T(1,128)} %param.6) | copy-start | bytes 676
  0.0 22.3 %copy-start = (bf16[8,1,7,128,128]{4,3,2,1,0:T(8,128)(2,1)S(1)}, bf16[8,1,7,128,128]{4,3,2,1,0:T(8,128)(2,1)}, u32[]{:S(2)}) copy-start(bf16[8,1,7,128,128]{4,3,2,1,0:T(8,128)(2,1)} %param.5) | copy-start | bytes 5505028
  0.0 1.4 %copy-start.1 = (bf16[8,4,128,128]{3,2,1,0:T(8,128)(2,1)S(1)}, bf16[8,4,128,128]{3,2,1,0:T(8,128)(2,1)}, u32[]{:S(2)}) copy-start(bf16[8,4,128,128]{3,2,1,0:T(8,128)(2,1)} %param.7) | copy-start | bytes 3145732
  1.4 26.7 %copy-start.2 = (s32[32,16]{0,1:T(8,128)S(1)}, s32[32,16]{0,1:T(8,128)}, u32[]{:S(2)}) copy-start(s32[32,16]{0,1:T(8,128)} %param.9) | copy-start | bytes 6148
